TPU v7x, 32 devices: a whole 2x2x4 slice. The times are simulated.
32 devices in a mesh: grp: 4 (over x, core), emb: 8 (over z, y).
Axes of the slice: x: 2, y: 2, z: 4, core: 2. Of those that a mesh axis runs over, the one named last changes fastest.
Arguments:
- indices: int32 [4, 8, 1024, 512], P(None, None, ('grp', 'emb')), may hold values from 0 to 255
- lengths: int32 [4, 1024, 512], P(None, ('grp', 'emb')), may hold values from 1 to 8
- dense: bfloat16 [4, 1024, 128], P(None, ('grp', 'emb')), may hold values from -6 to 6
- tables: bfloat16 [512, 256, 128], P('emb'), may hold values from -3 to 3
- project: bfloat16 [64, 513], replicated, may hold values from -0.25 to 0.25
- top_weight: bfloat16 [4096, 512], P('grp'), may hold values from -0.09375 to 0.09375
Outputs:
- scores: float32 [4, 1024, 512], P(None, ('grp', 'emb'))
Inputs may be any that keep to these rules, and one draw needn't show every extreme that they name: `indices`: a row of the table named by the last dimension; slots at or past the bag's length are ignored.
All inputs are finite; a program needn't handle non-finite values.
Results may differ from a plain program's by a relative error of at most 0.0085.
Values may be sent and summed in bfloat16 or wider, within the bound.
No kernel may reach another device: no remote copies, remote signals or barrier semaphores. Data moves between devices by JAX's collectives and lax.ppermute only.
A program may use at most 128 MiB of HBM per device.

v0:
```python
import functools
import jax
import jax.numpy as jnp
from jax import lax
from jax.experimental import pallas as pl
from jax.experimental.pallas import tpu as pltpu
from jax.sharding import PartitionSpec as P

FIELDS = 8
BITS = 4
PAD = 8
SPLIT = 5
VMEM = pl.BlockSpec(memory_space=pltpu.VMEM)
SMEM = pl.BlockSpec(memory_space=pltpu.SMEM)
ANY = pl.BlockSpec(memory_space=pl.ANY)


def params(mib):
    return pltpu.CompilerParams(vmem_limit_bytes=mib * 2**20)


def cost(us):
    return pl.CostEstimate(flops=int(us * 2e8), bytes_accessed=2**20, transcendentals=0)


def bag_kernel(line, side_ref, indices_ref, lengths_ref, kept_ref, sent_ref):
    micro, slots, _, table_count = indices_ref.shape
    tab_dev = table_count // line // 2
    side = side_ref[0]
    lengths = jnp.concatenate([lengths_ref[m] for m in range(micro)], axis=0)
    pairs = slots // 2
    for pair in range(pairs):
        words = []
        for slot in (pair, pair + pairs):
            picked = jnp.concatenate([indices_ref[m, slot] for m in range(micro)], axis=0)
            words.append(jnp.where(lengths > slot, picked, -1))
        turned = jnp.transpose((words[0] & 0xFFFF) | lax.shift_left(words[1], 16))
        for block in range(2 * line):
            value = turned[block * tab_dev : (block + 1) * tab_dev]
            rows = pl.ds(block // 2 * tab_dev * pairs + pair, tab_dev, stride=pairs)

            @pl.when(side == block % 2)
            def _():
                kept_ref[rows, :] = value

            @pl.when(side != block % 2)
            def _():
                sent_ref[rows, :] = value


def make_bags(side, indices, lengths, line):
    micro, slots, batch, table_count = indices.shape
    shape = jax.ShapeDtypeStruct((table_count // 2 * (slots // 2), micro * batch), jnp.int32)
    return pl.pallas_call(
        functools.partial(bag_kernel, line),
        out_shape=(shape, shape),
        in_specs=[SMEM, VMEM, VMEM],
        out_specs=(VMEM, VMEM),
        compiler_params=params(32),
        cost_estimate=cost(6),
        name="bags",
    )(side[None], indices, lengths)


def turn_kernel(cuts, member_ref, tables_ref, *refs):
    outs, (held, sem) = refs[: len(cuts)], refs[len(cuts) :]
    size = held.shape[0]
    copy = pltpu.make_async_copy(tables_ref.at[pl.ds(member_ref[0] * size, size)], held, sem)
    copy.start()
    copy.wait()
    for table in range(size):
        turned = jnp.transpose(held[table])
        for (first, part), out in zip(cuts, outs):
            out[table] = turned[first : first + part]


def turn_piece(member, tables, size, cuts):
    _, rows, width = tables.shape
    return pl.pallas_call(
        functools.partial(turn_kernel, cuts),
        out_shape=[jax.ShapeDtypeStruct((size, part, rows), tables.dtype) for _, part in cuts],
        in_specs=[SMEM, ANY],
        out_specs=[VMEM] * len(cuts),
        scratch_shapes=[pltpu.VMEM((size, rows, width), tables.dtype), pltpu.SemaphoreType.DMA(())],
        compiler_params=params(63),
        cost_estimate=cost(3),
        name="turn",
    )(member[None], tables)


def bag_counts(bag, rows):
    bag = jnp.concatenate(
        [lax.shift_right_arithmetic(lax.shift_left(bag, 16), 16), lax.shift_right_arithmetic(bag, 16)],
        axis=0,
    )
    slots, samples = bag.shape
    span = rows // FIELDS
    word = bag & (span - 1)
    shift = lax.shift_right_logical(bag, span.bit_length() - 1) * BITS
    step = jnp.where(bag >= 0, lax.shift_left(jnp.ones_like(bag), shift & 31), 0)
    ids = lax.broadcasted_iota(jnp.int32, (span, samples), 0)
    packed = jnp.zeros((span, samples), jnp.int32)
    for slot in range(slots):
        packed = packed + jnp.where(ids == word[slot : slot + 1], step[slot : slot + 1], 0)
    fields = [
        (lax.shift_right_logical(packed, BITS * field) & (2**BITS - 1)).astype(jnp.float32)
        for field in range(FIELDS)
    ]
    return jnp.concatenate([field.astype(jnp.bfloat16) for field in fields], axis=0)


def pool_kernel(first, blocks, pieces, size, unroll, earlier, own, places, *refs):
    sources = refs[: len(pieces)]
    bags_refs = refs[len(pieces) : len(pieces) + 2]
    refs = refs[len(pieces) + 2 :]
    before = refs[:earlier]
    refs = refs[earlier:]
    if earlier:
        project_ref, mine_ref, theirs_ref = refs[:3]
        tables_ref, bags, low_ref, high_ref, sems, sum_ref = refs[3:9]
        held = refs[9:]
        part = held[0].shape[0]
    else:
        (pooled_ref,) = refs[:1]
        tables_ref, bags, low_ref, high_ref, sems = refs[1:]
        part = pooled_ref.shape[0]
    count = tables_ref.shape[0]
    tab_dev = count // blocks
    rows = tables_ref.shape[1 if own else 2]
    samples = bags.shape[3]
    stride = count + PAD
    halves = (low_ref, high_ref)
    member = places[blocks]

    soon, later = [], []
    for number, source in enumerate(bags_refs):
        for block in range(blocks):
            rows_from = source.at[pl.ds(places[block] * tab_dev, tab_dev)]
            target = bags.at[number, pl.ds(block * tab_dev, tab_dev)]
            copy = pltpu.make_async_copy(rows_from, target, sems.at[number * blocks + block])
            (later if block else soon).append(copy)
    sem = 2 * blocks
    for source, (block, mask) in zip(sources, pieces):
        target = tables_ref.at[pl.ds(block * tab_dev + (member ^ mask) * size, size)]
        copy = pltpu.make_async_copy(source, target, sems.at[sem])
        (later if block or mask else soon).append(copy)
        sem += 1
    late = []
    for number, source in enumerate(before):
        columns = source.at[pl.ds(first if source.shape[0] != part else 0, part)]
        late.append(pltpu.make_async_copy(columns, held[number], sems.at[sem + number]))
    for copy in soon + later + late:
        copy.start()
    for copy in soon:
        copy.wait()

    base = member * size

    def some_tables(step, carry):
        if later:

            @pl.when(step == size // unroll)
            def _():
                for copy in later:
                    copy.wait()

        at = lax.rem(base + step * unroll, count)
        for inner in range(unroll):
            table = at + inner
            counts = jnp.concatenate(
                [bag_counts(bags[half, table], rows) for half in range(2)], axis=1
            )
            pooled = lax.dot_general(
                tables_ref[table],
                counts,
                (((0 if own else 1,), (0,)), ((), ())),
                preferred_element_type=jnp.float32,
            )
            for half in range(2):
                halves[half][pl.ds(table, part, stride=stride), :] = pooled[
                    :, half * samples : (half + 1) * samples
                ]
        return carry

    lax.fori_loop(0, count // unroll, some_tables, 0)

    if not earlier:

        def narrow(step, carry):
            for inner in range(4):
                column = step * 4 + inner
                start = pl.multiple_of(column * stride, PAD)
                for half in range(2):
                    value = halves[half][pl.ds(start, count), :].astype(jnp.bfloat16)
                    pooled_ref[column, :, half * samples : (half + 1) * samples] = value
            return carry

        lax.fori_loop(0, part // 4, narrow, 0)
        return

    outs = project_ref.shape[0]
    for copy in late:
        copy.wait()

    def some_columns(step, carry):
        for inner in range(4):
            column = step * 4 + inner
            start = pl.multiple_of(column * stride, PAD)
            here = [ref[pl.ds(start, count), :].astype(jnp.bfloat16) for ref in halves]
            pooled = jnp.concatenate(
                [ref[column] for ref in held] + [jnp.concatenate(here, axis=1)], axis=0
            )
            total = jnp.dot(project_ref[...], pooled, preferred_element_type=jnp.float32)
            mine_ref[pl.ds(column, outs, stride=part), :] = total[:, :samples]
            sum_ref[pl.ds(column, outs, stride=part), :] = total[:, samples:]
        return carry

    lax.fori_loop(0, part // 4, some_columns, 0)
    theirs_ref[...] = sum_ref[...].astype(theirs_ref.dtype)


def pool_blocks(places, sources, pieces, bags, tab_dev, part, first=0, earlier=(), project=None):
    own = project is None and sources[0].shape[0] == tab_dev
    blocks = places.shape[0] - 1
    count = blocks * tab_dev
    size = sources[0].shape[0]
    rows = sources[0].shape[1 if own else 2]
    _, pairs, samples = bags[0].shape
    scratch = [
        pltpu.VMEM((count, rows, part) if own else (count, part, rows), jnp.bfloat16),
        pltpu.VMEM((2, count, pairs, samples), jnp.int32),
        pltpu.VMEM((part * (count + PAD), samples), jnp.float32),
        pltpu.VMEM((part * (count + PAD), samples), jnp.float32),
        pltpu.SemaphoreType.DMA((2 * blocks + len(pieces) + len(earlier),)),
    ]
    if earlier:
        outs = project.shape[0]
        out_shape = (
            jax.ShapeDtypeStruct((outs * part, samples), jnp.float32),
            jax.ShapeDtypeStruct((outs * part, samples), jnp.bfloat16),
        )
        out_specs = (VMEM, VMEM)
        scratch += [pltpu.VMEM((outs * part, samples), jnp.float32)]
        scratch += [pltpu.VMEM((part, *one.shape[1:]), jnp.bfloat16) for one in earlier]
        more, specs = (project,), [VMEM]
    else:
        out_shape = jax.ShapeDtypeStruct((part, count, 2 * samples), jnp.bfloat16)
        out_specs, more, specs = VMEM, (), []
    unroll = min(16, size)
    return pl.pallas_call(
        functools.partial(pool_kernel, first, blocks, pieces, size, unroll, len(earlier), own),
        out_shape=out_shape,
        in_specs=[SMEM] + [ANY] * (len(sources) + 2 + len(earlier)) + specs,
        out_specs=out_specs,
        scratch_shapes=scratch,
        compiler_params=params(63),
        cost_estimate=cost(10),
        name="project" if earlier else "pool",
    )(places, *sources, *bags, *earlier, *more)


def score_kernel(masks, scale, member_ref, lead_ref, dense_ref, *refs):
    parts = len(refs) - len(masks) - 5
    sums = refs[:parts]
    top_parts = refs[parts : parts + len(masks)]
    scores_ref, turned, inter, top, sems = refs[parts + len(masks) :]
    own, back = sums[: parts // 2], sums[parts // 2 :]
    _, samples = dense_ref.shape
    outs = lead_ref.shape[0]
    half = outs // 2
    step_k, step_b = outs + PAD, samples + PAD
    copies = []
    for number, (mask, source) in enumerate(zip(masks, top_parts)):
        rows = source.shape[0]
        target = top.at[pl.ds((member_ref[0] ^ mask) * rows, rows)]
        copies.append(pltpu.make_async_copy(source, target, sems.at[number]))
    for copy in copies:
        copy.start()

    def compress(step, carry):
        for inner in range(4):
            k = step * 4 + inner
            columns = []
            for mine, theirs in zip(own, back):
                part = mine.shape[0] // outs
                rows = pl.ds(pl.multiple_of(k * part, part), part)
                columns.append(mine[rows, :] + theirs[rows, :].astype(jnp.float32))
            value = jnp.concatenate(columns, axis=0) + lead_ref[k] * dense_ref[...]
            value = jnp.transpose(value).astype(jnp.bfloat16).astype(jnp.float32)
            turned[pl.ds(k, samples, stride=step_k), :] = value
        return carry

    lax.fori_loop(0, outs // 4, compress, 0)

    def interact(step, carry):
        for inner in range(4):
            b = step * 4 + inner
            value = turned[pl.ds(pl.multiple_of(b * step_k, PAD), outs), :].astype(jnp.bfloat16)
            zero = jnp.zeros_like(value)
            left = jnp.concatenate([value[:half], value[half:]], axis=1)
            right = jnp.concatenate(
                [jnp.concatenate([value, zero], axis=1), jnp.concatenate([zero, value], axis=1)],
                axis=0,
            )
            pairs = lax.dot_general(
                left, right, (((1,), (1,)), ((), ())), preferred_element_type=jnp.float32
            )
            inter[pl.ds(b, half, stride=step_b), :] = pairs * scale
        return carry

    lax.fori_loop(0, samples // 4, interact, 0)
    for copy in copies:
        copy.wait()
    scores_ref[...] = jnp.zeros_like(scores_ref)

    def score(step, carry):
        left, right = [], []
        for inner in range(2):
            k = step * 2 + inner
            rows = pl.ds(pl.multiple_of(k * step_b, PAD), samples)
            left.append(inter[rows, :].astype(jnp.bfloat16))
            for high in range(2):
                start = pl.multiple_of((high * half + k) * outs, outs)
                right.append(top[pl.ds(start, outs), :])
        scores_ref[...] += jnp.dot(
            jnp.concatenate(left, axis=1),
            jnp.concatenate(right, axis=0),
            preferred_element_type=jnp.float32,
        )
        return carry

    lax.fori_loop(0, half // 2, score, 0)


def make_scores(place, lead, dense, own, back, tops, masks, top_shape):
    width, samples = dense.shape
    outs = lead.shape[0]
    return pl.pallas_call(
        functools.partial(score_kernel, masks, width ** (-0.5)),
        out_shape=jax.ShapeDtypeStruct((samples, top_shape[1]), jnp.float32),
        in_specs=[SMEM, SMEM, VMEM] + [VMEM] * (2 * len(own)) + [ANY] * len(tops),
        out_specs=VMEM,
        scratch_shapes=[
            pltpu.VMEM((samples * (outs + PAD), width), jnp.float32),
            pltpu.VMEM((outs // 2 * (samples + PAD), 2 * outs), jnp.float32),
            pltpu.VMEM(top_shape, jnp.bfloat16),
            pltpu.SemaphoreType.DMA((len(tops),)),
        ],
        compiler_params=params(40),
        cost_estimate=cost(20),
        name="scores",
    )(place, lead, dense, *own, *back, *tops)


def swap(value, axis, size, distance, keep=None, scale=1):
    pairs = []
    for a in range(size):
        if keep is None or keep(a, a ^ distance):
            pairs += [(a * scale + low, (a ^ distance) * scale + low) for low in range(scale)]
    return lax.ppermute(value, axis, pairs)


def routed_slot(distance):
    return distance >= 3 and distance % 2 == 1


def line_slot(value, slots, distance, line, position):
    if not routed_slot(distance):
        return swap(value, "emb", line, distance, None, 2)
    near = lambda a, b: abs(a - b) == 1
    direct = swap(value, "emb", line, distance, near, 2)
    far = lambda a, b: abs(b - (b ^ distance)) != 1
    routed = swap(slots[distance - 2], "emb", line, 1, far, 2)
    adjacent = jnp.abs(position - (position ^ distance)) == 1
    return jnp.where(adjacent, direct, routed)


def share(value, size):
    pieces, masks = [value], [0]
    for bit in bits_of(size):
        moved = [swap(piece, "grp", size, bit) for piece in pieces]
        pieces, masks = pieces + moved, masks + [mask ^ bit for mask in masks]
    return pieces, masks


def bits_of(size):
    return [2**power for power in range(size.bit_length() - 2, -1, -1)]


def chunk_widths(width, piece):
    return (width // 8 * SPLIT, width - width // 8 * SPLIT) if piece >= 4096 else (width,)


def shards(grp, emb, indices, lengths, dense, tables, project, top_weight):
    micro, slot_count, batch, _ = indices.shape
    tab_dev, rows, width = tables.shape
    outs = project.shape[0]
    samples = micro * batch
    line = emb // 2
    place = lax.axis_index("emb").astype(jnp.int32)
    member = lax.axis_index("grp").astype(jnp.int32)
    position, side = place // 2, place % 2
    size = tab_dev // grp
    cuts, first = [], 0
    for part in chunk_widths(width, size * rows):
        cuts.append((first, part))
        first += part
    sends = turn_piece(member, tables, size, cuts)

    top_rows = top_weight.shape[0]
    tops, top_masks = [top_weight], [0]
    for bit in bits_of(grp):
        moved = [swap(piece, "grp", grp, bit) for piece in tops]
        tops, top_masks = tops + moved, top_masks + [mask ^ bit for mask in top_masks]

    kept, sent = make_bags(side, indices, lengths, line)
    got = swap(sent, "emb", emb, 1)
    bags = [bag.reshape(line * tab_dev, slot_count // 2, samples) for bag in (kept, got)]

    mixing = project[:, 1:].reshape(outs, line, 2, tab_dev)
    mixing = lax.dynamic_index_in_dim(mixing, side, 2, keepdims=False)
    order = position ^ jnp.arange(line)
    mixing = jnp.take(mixing, order, axis=1).reshape(outs, line * tab_dev)

    where = jnp.stack([position, member * 0])
    near = pool_blocks(where, [tables], [(0, 0)], bags, tab_dev, width)
    own, back = [], []
    for (first, part), send in zip(cuts, sends):
        slots, sources, pieces = [], [], []
        for distance in range(1, line):
            slots.append(line_slot(send, slots, distance, line, position))
            shared, masks = share(slots[-1], grp)
            sources.append(shared)
            pieces.append([(0 if distance == line - 1 else distance - 1, mask) for mask in masks])
        pooled = [near]
        if line > 2:
            where = jnp.concatenate([order[1 : line - 1], member[None]]).astype(jnp.int32)
            pooled.append(
                pool_blocks(where, sum(sources[:-1], []), sum(pieces[:-1], []), bags, tab_dev, part)
            )
        where = jnp.stack([order[line - 1], member]).astype(jnp.int32)
        mine_sum, their_sum = pool_blocks(
            where, sources[-1], pieces[-1], bags, tab_dev, part, first, tuple(pooled), mixing
        )
        own.append(mine_sum)
        back.append(swap(their_sum, "emb", emb, 1))

    flat_dense = jnp.transpose(dense.reshape(samples, width)).astype(jnp.float32)
    lead = project[:, 0].astype(jnp.float32)
    top_shape = (top_rows * grp, top_weight.shape[1])
    scores = make_scores(
        member[None], lead, flat_dense, own, back, tops, tuple(top_masks), top_shape
    )
    return scores.reshape(micro, batch, -1)


def solution(mesh):
    placed = (
        P(None, None, ("grp", "emb"), None),
        P(None, ("grp", "emb"), None),
        P(None, ("grp", "emb"), None),
        P("emb", None, None),
        P(),
        P("grp", None),
    )
    grp, emb = mesh.shape["grp"], mesh.shape["emb"]

    def body(*args):
        return shards(grp, emb, *args)

    step = jax.shard_map(
        body, mesh=mesh, in_specs=placed, out_specs=P(None, ("grp", "emb"), None), check_vma=False
    )

    def run(indices, lengths, dense, tables, project, top_weight):
        args = (indices, lengths, dense, tables, project, top_weight)
        return step(*args)

    return run
```

profile of v0, /device:TPU:0, one launch (start us, length us, event | category | flops | bytes accessed | tf_op | source)
XLA Modules:
  0.0 255.7 jit_solution(12016977697310109841)
XLA Ops:
  0.0 2.6 %turn.1 = (bf16[16,80,256]{2,1,0:T(8,128)(2,1)}, bf16[16,48,256]{2,1,0:T(8,128)(2,1)}) custom-call(s32[1]{0:T(128)} %bitcast.member_ref, bf16[64,256,128]{2,1,0:T(8,128)(2,1)} %refs_0_.1), custom_call_target="tpu_custom_call" | custom-call | flops 600000000 | bytes 1048576 | tf_op jit(solution)/shard_map/turn/pallas_call | solution.py:79
  2.6 0.7 collective-permute-start.14
  3.3 5.8 %collective-permute-start.1 = (bf16[16,80,256]{2,1,0:T(8,128)(2,1)}, bf16[16,80,256]{2,1,0:T(8,128)(2,1)S(1)}, u32[]{:S(2)}, u32[]{:S(2)}) collective-permute-start(bf16[16,80,256]{2,1,0:T(8,128)(2,1)} %get-tuple-element.13), channel_id=1, source_target_pairs={{0,4},{1,5},{2,6},{3,7},{4,0},{5,1},{6,2},{7,3},{8,12},{9,13},{10,... | collective-permute-start | bytes 1966088 | tf_op jit(solution)/shard_map/ppermute | solution.py:360
  9.1 3.0 %collective-permute-start.20 = (bf16[16,48,256]{2,1,0:T(8,128)(2,1)}, bf16[16,48,256]{2,1,0:T(8,128)(2,1)}, u32[]{:S(2)}, u32[]{:S(2)}) collective-permute-start(bf16[16,48,256]{2,1,0:T(8,128)(2,1)} %get-tuple-element.17), channel_id=1, source_target_pairs={{0,2},{1,3},{2,0},{3,1},{4,6},{5,7},{6,4},{7,5},{8,10},{9,11},{10,... | collective-permute-start | bytes 1179656 | tf_op jit(solution)/shard_map/ppermute | solution.py:360
  12.1 1.5 collective-permute-start
  13.6 1.6 copy-done.2
  15.2 0.7 bags.1
  15.9 0.8 copy-done
  16.8 1.5 collective-permute-start.6
  18.3 45.9 %collective-permute-done.15.refs_4_ = bf16[16,48,256]{2,1,0:T(8,128)(2,1)} collective-permute-done((bf16[16,48,256]{2,1,0:T(8,128)(2,1)}, bf16[16,48,256]{2,1,0:T(8,128)(2,1)}, u32[]{:S(2)}, u32[]{:S(2)}) %collective-permute-start.15) | collective-permute-done | bytes 393248 | tf_op jit(solution)/shard_map/ppermute | solution.py:360
  64.2 1.3 collective-permute-start.16
  65.5 2.7 %collective-permute-start.7 = (bf16[16,80,256]{2,1,0:T(8,128)(2,1)}, bf16[16,80,256]{2,1,0:T(8,128)(2,1)S(1)}, u32[]{:S(2)}, u32[]{:S(2)}) collective-permute-start(bf16[16,80,256]{2,1,0:T(8,128)(2,1)} %get-tuple-element.13), channel_id=1, source_target_pairs={{0,2},{1,3},{2,0},{3,1},{4,6},{5,7},{6,4},{7,5},{8,10},{9,11},{10,... | collective-permute-start | bytes 1966088 | tf_op jit(solution)/shard_map/ppermute | solution.py:360
  68.2 1.3 collective-permute-start.2
  69.5 1.6 collective-permute-start.21
  71.1 7.2 %collective-permute-done.16 = bf16[16,48,256]{2,1,0:T(8,128)(2,1)S(1)} collective-permute-done((bf16[16,48,256]{2,1,0:T(8,128)(2,1)}, bf16[16,48,256]{2,1,0:T(8,128)(2,1)S(1)}, u32[]{:S(2)}, u32[]{:S(2)}) %collective-permute-start.16) | collective-permute-done | bytes 393248 | tf_op jit(solution)/shard_map/ppermute | solution.py:360
  78.3 1.5 collective-permute-start.24
  79.8 12.5 %collective-permute-done.7.refs_0_ = bf16[16,80,256]{2,1,0:T(8,128)(2,1)S(1)} collective-permute-done((bf16[16,80,256]{2,1,0:T(8,128)(2,1)}, bf16[16,80,256]{2,1,0:T(8,128)(2,1)S(1)}, u32[]{:S(2)}, u32[]{:S(2)}) %collective-permute-start.7) | collective-permute-done | bytes 655392 | tf_op jit(solution)/shard_map/ppermute | solution.py:360
  92.3 1.6 collective-permute-start.17
  93.9 0.7 slice.15
  94.6 0.5 collective-permute-start.8
  95.2 8.2 %collective-permute-done.2 = bf16[16,80,256]{2,1,0:T(8,128)(2,1)} collective-permute-done((bf16[16,80,256]{2,1,0:T(8,128)(2,1)S(1)}, bf16[16,80,256]{2,1,0:T(8,128)(2,1)}, u32[]{:S(2)}, u32[]{:S(2)}) %collective-permute-start.2) | collective-permute-done | bytes 655392 | tf_op jit(solution)/shard_map/ppermute | solution.py:360
  103.3 1.5 collective-permute-start.11
  104.8 2.0 broadcast_select_fusion.refs_0_
  106.9 0.6 collective-permute-start.3
  107.5 1.3 pad_add_fusion.places
  108.8 9.7 %collective-permute-done.8.refs_1_ = bf16[16,80,256]{2,1,0:T(8,128)(2,1)} collective-permute-done((bf16[16,80,256]{2,1,0:T(8,128)(2,1)S(1)}, bf16[16,80,256]{2,1,0:T(8,128)(2,1)}, u32[]{:S(2)}, u32[]{:S(2)}) %collective-permute-start.8) | collective-permute-done | bytes 655392 | tf_op jit(solution)/shard_map/ppermute | solution.py:360
  118.5 1.5 collective-permute-start.29
  120.0 12.5 %collective-permute-done.11.refs_5_ = bf16[16,80,256]{2,1,0:T(8,128)(2,1)} collective-permute-done((bf16[16,80,256]{2,1,0:T(8,128)(2,1)S(1)}, bf16[16,80,256]{2,1,0:T(8,128)(2,1)}, u32[]{:S(2)}, u32[]{:S(2)}) %collective-permute-start.11) | collective-permute-done | bytes 655392 | tf_op jit(solution)/shard_map/ppermute | solution.py:360
  132.6 0.7 pad_add_fusion.2.places
  133.6 0.6 collective-permute-start.4
  134.2 12.4 %collective-permute-done.3.refs_1_ = bf16[16,80,256]{2,1,0:T(8,128)(2,1)} collective-permute-done((bf16[16,80,256]{2,1,0:T(8,128)(2,1)}, bf16[16,80,256]{2,1,0:T(8,128)(2,1)}, u32[]{:S(2)}, u32[]{:S(2)}) %collective-permute-start.3) | collective-permute-done | bytes 655392 | tf_op jit(solution)/shard_map/ppermute | solution.py:360
  146.6 0.6 pad_add_fusion.1.places
  147.2 0.6 gather_fusion
  148.1 0.6 broadcast_select_fusion.2.refs_8_
  148.8 11.5 %pool.3.refs_6_ = bf16[128,64,256]{2,1,0:T(8,128)(2,1)} custom-call(s32[2]{0:T(128)} %pad_add_fusion.1.places, bf16[64,256,128]{2,1,0:T(8,128)(2,1)} %refs_0_.1, s32[256,4,128]{2,1,0:T(4,128)} %bitcast.16, s32[256,4,128]{2,1,0:T(4,128)} %bitcast.22), custom_call_target="tpu_custom_call" | custom-call | flops 2000000000 | bytes 1048576 | tf_op jit(solution)/shard_map/pool/pallas_call | solution.py:250
  160.3 0.6 collective-permute-start.23
  160.9 15.5 %pool.4.refs_7_ = bf16[80,128,256]{2,1,0:T(8,128)(2,1)} custom-call(s32[3]{0:T(128)} %pad_add_fusion.2.places, bf16[16,80,256]{2,1,0:T(8,128)(2,1)} %copy-done.8, bf16[16,80,256]{2,1,0:T(8,128)(2,1)} %collective-permute-done.8.refs_1_, bf16[16,80,256]{2,1,0:T(8,128)(2,1)} %copy-done.9, bf16[16,80,256]{2,1,0:T(8,128)(2,1)} %collective-permute-done.10.refs_3_, ...), custom_call_target="tpu_custom_call" | custom-call | flops 2000000000 | bytes 1048576 | tf_op jit(solution)/shard_map/pool/pallas_call | solution.py:250
  176.4 0.5 collective-permute-start.18
  177.0 13.8 %project.2 = (f32[5120,128]{1,0:T(8,128)}, bf16[5120,128]{1,0:T(8,128)(2,1)}) custom-call(s32[2]{0:T(128)} %pad_add_fusion.places, bf16[16,80,256]{2,1,0:T(8,128)(2,1)} %broadcast_select_fusion.refs_0_, bf16[16,80,256]{2,1,0:T(8,128)(2,1)} %collective-permute-done.3.refs_1_, bf16[16,80,256]{2,1,0:T(8,128)(2,1)} %collective-permute-done.4.refs_2_, ...), custom_call_target="tpu_custom_call" | custom-call | flops 2000000000 | bytes 1048576 | tf_op jit(solution)/shard_map/project/pallas_call | solution.py:250
  190.9 1.6 collective-permute-start.27
  193.0 14.2 %pool.5.refs_7_ = bf16[48,128,256]{2,1,0:T(8,128)(2,1)} custom-call(s32[3]{0:T(128)} %pad_add_fusion.2.places, bf16[16,48,256]{2,1,0:T(8,128)(2,1)} %collective-permute-done.20.refs_0_, bf16[16,48,256]{2,1,0:T(8,128)(2,1)} %collective-permute-done.21.refs_1_, bf16[16,48,256]{2,1,0:T(8,128)(2,1)} %collective-permute-done.22.refs_2_, ...), custom_call_target="tpu_custom_call" | custom-call | flops 2000000000 | bytes 1048576 | tf_op jit(solution)/shard_map/pool/pallas_call | solution.py:250
  207.2 11.2 %project.3 = (f32[3072,128]{1,0:T(8,128)}, bf16[3072,128]{1,0:T(8,128)(2,1)}) custom-call(s32[2]{0:T(128)} %pad_add_fusion.places, bf16[16,48,256]{2,1,0:T(8,128)(2,1)} %copy-done.6, bf16[16,48,256]{2,1,0:T(8,128)(2,1)} %copy-done.10, bf16[16,48,256]{2,1,0:T(8,128)(2,1)} %collective-permute-done.18.refs_2_, ...), custom_call_target="tpu_custom_call" | custom-call | flops 2000000000 | bytes 1048576 | tf_op jit(solution)/shard_map/project/pallas_call | solution.py:250
  218.5 0.6 collective-permute-start.28
  219.1 0.8 convert_reduce_fusion.lead_ref
  220.0 19.1 %collective-permute-done.28.refs_3_ = bf16[3072,128]{1,0:T(8,128)(2,1)S(1)} collective-permute-done((bf16[3072,128]{1,0:T(8,128)(2,1)}, bf16[3072,128]{1,0:T(8,128)(2,1)S(1)}, u32[]{:S(2)}, u32[]{:S(2)}) %collective-permute-start.28) | collective-permute-done | bytes 786464 | tf_op jit(solution)/shard_map/ppermute | solution.py:360
  239.1 1.7 copy-done.1
  240.8 1.4 copy-done.3
  242.2 13.5 %scores.1 = f32[128,512]{1,0:T(8,128)} custom-call(s32[1]{0:T(128)} %bitcast.member_ref, f32[64]{0:T(128)S(1)} %convert_reduce_fusion.lead_ref, f32[128,128]{1,0:T(8,128)S(1)} %bitcast.21, f32[5120,128]{1,0:T(8,128)S(1)} %copy-done.1, f32[3072,128]{1,0:T(8,128)S(1)} %copy-done.3, bf16[5120,128]{1,0:T(8,128)(2,1)} %collective-permute-done.27.refs_2_, ...), custom_call_target="tpu_custom_call" | custom-call | flops 4000000000 | bytes 1048576 | tf_op jit(solution)/shard_map/scores/pallas_call | solution.py:338
  (78 shorter events, 1.8 us)
Async XLA Ops:
  0.0 13.6 %copy-start.4 = (s32[4,32,512]{2,1,0:T(8,128)S(1)}, s32[4,32,512]{2,1,0:T(8,128)}, u32[]{:S(2)}) copy-start(s32[4,32,512]{2,1,0:T(8,128)} %lengths_ref.1) | copy-start | bytes 786436
  2.6 14.2 %collective-permute-start.14 = (bf16[16,48,256]{2,1,0:T(8,128)(2,1)}, bf16[16,48,256]{2,1,0:T(8,128)(2,1)S(1)}, u32[]{:S(2)}, u32[]{:S(2)}) collective-permute-start(bf16[16,48,256]{2,1,0:T(8,128)(2,1)} %get-tuple-element.17), channel_id=1, source_target_pairs={{2,4},{3,5},{4,2},{5,3},{10,12},{11,13},{12,10},{13,11},{18,20},{1... | collective-permute-start | bytes 1179656 | tf_op jit(solution)/shard_map/ppermute | solution.py:360
  3.3 65.0 %collective-permute-start.1 = (bf16[16,80,256]{2,1,0:T(8,128)(2,1)}, bf16[16,80,256]{2,1,0:T(8,128)(2,1)S(1)}, u32[]{:S(2)}, u32[]{:S(2)}) collective-permute-start(bf16[16,80,256]{2,1,0:T(8,128)(2,1)} %get-tuple-element.13), channel_id=1, source_target_pairs={{0,4},{1,5},{2,6},{3,7},{4,0},{5,1},{6,2},{7,3},{8,12},{9,13},{10,... | collective-permute-start | bytes 1966088 | tf_op jit(solution)/shard_map/ppermute | solution.py:360
  9.1 55.1 %collective-permute-start.15 = (bf16[16,48,256]{2,1,0:T(8,128)(2,1)}, bf16[16,48,256]{2,1,0:T(8,128)(2,1)}, u32[]{:S(2)}, u32[]{:S(2)}) collective-permute-start(bf16[16,48,256]{2,1,0:T(8,128)(2,1)} %get-tuple-element.17), channel_id=1, source_target_pairs={{0,4},{1,5},{2,6},{3,7},{4,0},{5,1},{6,2},{7,3},{8,12},{9,13},{10,... | collective-permute-start | bytes 1179656 | tf_op jit(solution)/shard_map/ppermute | solution.py:360
  9.1 56.3 %collective-permute-start.20 = (bf16[16,48,256]{2,1,0:T(8,128)(2,1)}, bf16[16,48,256]{2,1,0:T(8,128)(2,1)}, u32[]{:S(2)}, u32[]{:S(2)}) collective-permute-start(bf16[16,48,256]{2,1,0:T(8,128)(2,1)} %get-tuple-element.17), channel_id=1, source_target_pairs={{0,2},{1,3},{2,0},{3,1},{4,6},{5,7},{6,4},{7,5},{8,10},{9,11},{10,... | collective-permute-start | bytes 1179656 | tf_op jit(solution)/shard_map/ppermute | solution.py:360
  12.1 59.0 %collective-permute-start = (bf16[16,80,256]{2,1,0:T(8,128)(2,1)}, bf16[16,80,256]{2,1,0:T(8,128)(2,1)}, u32[]{:S(2)}, u32[]{:S(2)}) collective-permute-start(bf16[16,80,256]{2,1,0:T(8,128)(2,1)} %get-tuple-element.13), channel_id=1, source_target_pairs={{2,4},{3,5},{4,2},{5,3},{10,12},{11,13},{12,10},{13,11},{18,20},{1... | collective-permute-start | bytes 1966088 | tf_op jit(solution)/shard_map/ppermute | solution.py:360
  13.6 1.6 copy-start.2
  15.9 0.8 copy-start
  16.7 116.5 %copy-start.12 = (bf16[64,513]{1,0:T(8,128)(2,1)S(1)}, bf16[64,513]{1,0:T(8,128)(2,1)}, u32[]{:S(2)}) copy-start(bf16[64,513]{1,0:T(8,128)(2,1)} %param.10) | copy-start | bytes 196996
  16.8 52.8 %collective-permute-start.6 = (s32[1024,128]{1,0:T(8,128)S(1)}, s32[1024,128]{1,0:T(8,128)S(1)}, u32[]{:S(2)}, u32[]{:S(2)}) collective-permute-start(s32[1024,128]{1,0:T(8,128)S(1)} %get-tuple-element.15), channel_id=1, source_target_pairs={{0,1},{1,0},{2,3},{3,2},{4,5},{5,4},{6,7},{7,6},{8,9},{9,8},{10,11... | collective-permute-start | bytes 1572872 | tf_op jit(solution)/shard_map/ppermute | solution.py:360
  64.2 14.1 %collective-permute-start.16 = (bf16[16,48,256]{2,1,0:T(8,128)(2,1)}, bf16[16,48,256]{2,1,0:T(8,128)(2,1)S(1)}, u32[]{:S(2)}, u32[]{:S(2)}) collective-permute-start(bf16[16,48,256]{2,1,0:T(8,128)(2,1)} %collective-permute-done.15.refs_4_), channel_id=1, source_target_pairs={{2,0},{3,1},{4,6},{5,7},{10,8},{11,9},{12,14},{13,15},{18,16},{19,... | collective-permute-start | bytes 1179656 | tf_op jit(solution)/shard_map/ppermute | solution.py:360
  65.5 26.8 %collective-permute-start.7 = (bf16[16,80,256]{2,1,0:T(8,128)(2,1)}, bf16[16,80,256]{2,1,0:T(8,128)(2,1)S(1)}, u32[]{:S(2)}, u32[]{:S(2)}) collective-permute-start(bf16[16,80,256]{2,1,0:T(8,128)(2,1)} %get-tuple-element.13), channel_id=1, source_target_pairs={{0,2},{1,3},{2,0},{3,1},{4,6},{5,7},{6,4},{7,5},{8,10},{9,11},{10,... | collective-permute-start | bytes 1966088 | tf_op jit(solution)/shard_map/ppermute | solution.py:360
  68.2 38.7 %copy-start.7 = (bf16[16,80,256]{2,1,0:T(8,128)(2,1)}, bf16[16,80,256]{2,1,0:T(8,128)(2,1)S(1)}, u32[]{:S(2)}) copy-start(bf16[16,80,256]{2,1,0:T(8,128)(2,1)S(1)} %collective-permute-done.1.refs_4_) | copy-start | bytes 1966084
  68.2 35.1 %collective-permute-start.2 = (bf16[16,80,256]{2,1,0:T(8,128)(2,1)S(1)}, bf16[16,80,256]{2,1,0:T(8,128)(2,1)}, u32[]{:S(2)}, u32[]{:S(2)}) collective-permute-start(bf16[16,80,256]{2,1,0:T(8,128)(2,1)S(1)} %collective-permute-done.1.refs_4_), channel_id=1, source_target_pairs={{2,0},{3,1},{4,6},{5,7},{10,8},{11,9},{12,14},{13,15},{18,16},{19,... | collective-permute-start | bytes 1966088 | tf_op jit(solution)/shard_map/ppermute | solution.py:360
  69.5 79.2 %copy-start.5 = (s32[1024,128]{1,0:T(8,128)}, s32[1024,128]{1,0:T(8,128)S(1)}, u32[]{:S(2)}) copy-start(s32[1024,128]{1,0:T(8,128)S(1)} %collective-permute-done.6) | copy-start | bytes 1572868
  69.5 22.8 %collective-permute-start.21 = (bf16[16,48,256]{2,1,0:T(8,128)(2,1)}, bf16[16,48,256]{2,1,0:T(8,128)(2,1)}, u32[]{:S(2)}, u32[]{:S(2)}) collective-permute-start(bf16[16,48,256]{2,1,0:T(8,128)(2,1)} %collective-permute-done.20.refs_0_), channel_id=1, source_target_pairs={{0,16},{8,24},{16,0},{24,8},{1,17},{9,25},{17,1},{25,9},{2,18},{10... | collective-permute-start | bytes 1179656 | tf_op jit(solution)/shard_map/ppermute | solution.py:360
  71.1 23.5 %collective-permute-start.22 = (bf16[16,48,256]{2,1,0:T(8,128)(2,1)}, bf16[16,48,256]{2,1,0:T(8,128)(2,1)}, u32[]{:S(2)}, u32[]{:S(2)}) collective-permute-start(bf16[16,48,256]{2,1,0:T(8,128)(2,1)} %collective-permute-done.20.refs_0_), channel_id=1, source_target_pairs={{0,8},{8,0},{16,24},{24,16},{1,9},{9,1},{17,25},{25,17},{2,10},{10... | collective-permute-start | bytes 1179656 | tf_op jit(solution)/shard_map/ppermute | solution.py:360
  78.3 16.9 %collective-permute-start.24 = (bf16[16,48,256]{2,1,0:T(8,128)(2,1)}, bf16[16,48,256]{2,1,0:T(8,128)(2,1)}, u32[]{:S(2)}, u32[]{:S(2)}) collective-permute-start(bf16[16,48,256]{2,1,0:T(8,128)(2,1)} %collective-permute-done.15.refs_4_), channel_id=1, source_target_pairs={{0,16},{8,24},{16,0},{24,8},{1,17},{9,25},{17,1},{25,9},{2,18},{10... | collective-permute-start | bytes 1179656 | tf_op jit(solution)/shard_map/ppermute | solution.py:360
  79.8 96.6 %copy-start.6 = (bf16[16,48,256]{2,1,0:T(8,128)(2,1)}, bf16[16,48,256]{2,1,0:T(8,128)(2,1)S(1)}, u32[]{:S(2)}) copy-start(bf16[16,48,256]{2,1,0:T(8,128)(2,1)S(1)} %broadcast_select_fusion.1.refs_0_) | copy-start | bytes 1179652
  92.3 41.3 %copy-start.8 = (bf16[16,80,256]{2,1,0:T(8,128)(2,1)}, bf16[16,80,256]{2,1,0:T(8,128)(2,1)S(1)}, u32[]{:S(2)}) copy-start(bf16[16,80,256]{2,1,0:T(8,128)(2,1)S(1)} %collective-permute-done.7.refs_0_) | copy-start | bytes 1966084
  92.3 14.5 %collective-permute-start.25 = (bf16[16,48,256]{2,1,0:T(8,128)(2,1)}, bf16[16,48,256]{2,1,0:T(8,128)(2,1)S(1)}, u32[]{:S(2)}, u32[]{:S(2)}) collective-permute-start(bf16[16,48,256]{2,1,0:T(8,128)(2,1)} %collective-permute-done.15.refs_4_), channel_id=1, source_target_pairs={{0,8},{8,0},{16,24},{24,16},{1,9},{9,1},{17,25},{25,17},{2,10},{10... | collective-permute-start | bytes 1179656 | tf_op jit(solution)/shard_map/ppermute | solution.py:360
  92.3 14.6 %collective-permute-start.17 = (bf16[16,48,256]{2,1,0:T(8,128)(2,1)S(1)}, bf16[16,48,256]{2,1,0:T(8,128)(2,1)S(1)}, u32[]{:S(2)}, u32[]{:S(2)}) collective-permute-start(bf16[16,48,256]{2,1,0:T(8,128)(2,1)S(1)} %broadcast_select_fusion.1.refs_0_), channel_id=1, source_target_pairs={{0,16},{8,24},{16,0},{24,8},{1,17},{9,25},{17,1},{25,9},{2,18},{10... | collective-permute-start | bytes 1179656 | tf_op jit(solution)/shard_map/ppermute | solution.py:360
  94.6 23.9 %collective-permute-start.8 = (bf16[16,80,256]{2,1,0:T(8,128)(2,1)S(1)}, bf16[16,80,256]{2,1,0:T(8,128)(2,1)}, u32[]{:S(2)}, u32[]{:S(2)}) collective-permute-start(bf16[16,80,256]{2,1,0:T(8,128)(2,1)S(1)} %collective-permute-done.7.refs_0_), channel_id=1, source_target_pairs={{0,16},{8,24},{16,0},{24,8},{1,17},{9,25},{17,1},{25,9},{2,18},{10... | collective-permute-start | bytes 1966088 | tf_op jit(solution)/shard_map/ppermute | solution.py:360
  95.2 24.9 %collective-permute-start.9 = (bf16[16,80,256]{2,1,0:T(8,128)(2,1)S(1)}, bf16[16,80,256]{2,1,0:T(8,128)(2,1)S(1)}, u32[]{:S(2)}, u32[]{:S(2)}) collective-permute-start(bf16[16,80,256]{2,1,0:T(8,128)(2,1)S(1)} %collective-permute-done.7.refs_0_), channel_id=1, source_target_pairs={{0,8},{8,0},{16,24},{24,16},{1,9},{9,1},{17,25},{25,17},{2,10},{10... | collective-permute-start | bytes 1966088 | tf_op jit(solution)/shard_map/ppermute | solution.py:360
  103.3 29.2 %collective-permute-start.11 = (bf16[16,80,256]{2,1,0:T(8,128)(2,1)S(1)}, bf16[16,80,256]{2,1,0:T(8,128)(2,1)}, u32[]{:S(2)}, u32[]{:S(2)}) collective-permute-start(bf16[16,80,256]{2,1,0:T(8,128)(2,1)S(1)} %collective-permute-done.1.refs_4_), channel_id=1, source_target_pairs={{0,16},{8,24},{16,0},{24,8},{1,17},{9,25},{17,1},{25,9},{2,18},{10... | collective-permute-start | bytes 1966088 | tf_op jit(solution)/shard_map/ppermute | solution.py:360
  106.9 25.7 %copy-start.14 = (bf16[16,48,256]{2,1,0:T(8,128)(2,1)}, bf16[16,48,256]{2,1,0:T(8,128)(2,1)S(1)}, u32[]{:S(2)}) copy-start(bf16[16,48,256]{2,1,0:T(8,128)(2,1)S(1)} %collective-permute-done.25.refs_6_) | copy-start | bytes 1179652
  106.9 26.8 %collective-permute-start.12 = (bf16[16,80,256]{2,1,0:T(8,128)(2,1)S(1)}, bf16[16,80,256]{2,1,0:T(8,128)(2,1)}, u32[]{:S(2)}, u32[]{:S(2)}) collective-permute-start(bf16[16,80,256]{2,1,0:T(8,128)(2,1)S(1)} %collective-permute-done.1.refs_4_), channel_id=1, source_target_pairs={{0,8},{8,0},{16,24},{24,16},{1,9},{9,1},{17,25},{25,17},{2,10},{10... | collective-permute-start | bytes 1966088 | tf_op jit(solution)/shard_map/ppermute | solution.py:360
  106.9 26.3 %copy-start.10 = (bf16[16,48,256]{2,1,0:T(8,128)(2,1)}, bf16[16,48,256]{2,1,0:T(8,128)(2,1)S(1)}, u32[]{:S(2)}) copy-start(bf16[16,48,256]{2,1,0:T(8,128)(2,1)S(1)} %collective-permute-done.17.refs_1_) | copy-start | bytes 1179652
  106.9 39.7 %collective-permute-start.3 = (bf16[16,80,256]{2,1,0:T(8,128)(2,1)}, bf16[16,80,256]{2,1,0:T(8,128)(2,1)}, u32[]{:S(2)}, u32[]{:S(2)}) collective-permute-start(bf16[16,80,256]{2,1,0:T(8,128)(2,1)} %broadcast_select_fusion.refs_0_), channel_id=1, source_target_pairs={{0,16},{8,24},{16,0},{24,8},{1,17},{9,25},{17,1},{25,9},{2,18},{10... | collective-permute-start | bytes 1966088 | tf_op jit(solution)/shard_map/ppermute | solution.py:360
  118.5 72.3 %collective-permute-start.29 = (bf16[1024,512]{1,0:T(8,128)(2,1)}, bf16[1024,512]{1,0:T(8,128)(2,1)}, u32[]{:S(2)}, u32[]{:S(2)}) collective-permute-start(bf16[1024,512]{1,0:T(8,128)(2,1)} %refs_4_.1), channel_id=1, source_target_pairs={{0,16},{8,24},{16,0},{24,8},{1,17},{9,25},{17,1},{25,9},{2,18},{10... | collective-permute-start | bytes 3145736 | tf_op jit(solution)/shard_map/ppermute | solution.py:360
  120.0 14.2 %copy-start.9 = (bf16[16,80,256]{2,1,0:T(8,128)(2,1)}, bf16[16,80,256]{2,1,0:T(8,128)(2,1)S(1)}, u32[]{:S(2)}) copy-start(bf16[16,80,256]{2,1,0:T(8,128)(2,1)S(1)} %collective-permute-done.9.refs_2_) | copy-start | bytes 1966084
  120.0 40.2 %collective-permute-start.10 = (bf16[16,80,256]{2,1,0:T(8,128)(2,1)}, bf16[16,80,256]{2,1,0:T(8,128)(2,1)}, u32[]{:S(2)}, u32[]{:S(2)}) collective-permute-start(bf16[16,80,256]{2,1,0:T(8,128)(2,1)} %collective-permute-done.8.refs_1_), channel_id=1, source_target_pairs={{0,8},{8,0},{16,24},{24,16},{1,9},{9,1},{17,25},{25,17},{2,10},{10... | collective-permute-start | bytes 1966088 | tf_op jit(solution)/shard_map/ppermute | solution.py:360
  132.6 28.3 %collective-permute-start.13 = (bf16[16,80,256]{2,1,0:T(8,128)(2,1)}, bf16[16,80,256]{2,1,0:T(8,128)(2,1)}, u32[]{:S(2)}, u32[]{:S(2)}) collective-permute-start(bf16[16,80,256]{2,1,0:T(8,128)(2,1)} %collective-permute-done.11.refs_5_), channel_id=1, source_target_pairs={{0,8},{8,0},{16,24},{24,16},{1,9},{9,1},{17,25},{25,17},{2,10},{10... | collective-permute-start | bytes 1966088 | tf_op jit(solution)/shard_map/ppermute | solution.py:360
  133.6 42.8 %collective-permute-start.4 = (bf16[16,80,256]{2,1,0:T(8,128)(2,1)}, bf16[16,80,256]{2,1,0:T(8,128)(2,1)}, u32[]{:S(2)}, u32[]{:S(2)}) collective-permute-start(bf16[16,80,256]{2,1,0:T(8,128)(2,1)} %broadcast_select_fusion.refs_0_), channel_id=1, source_target_pairs={{0,8},{8,0},{16,24},{24,16},{1,9},{9,1},{17,25},{25,17},{2,10},{10... | collective-permute-start | bytes 1966088 | tf_op jit(solution)/shard_map/ppermute | solution.py:360
  146.6 30.3 %collective-permute-start.5 = (bf16[16,80,256]{2,1,0:T(8,128)(2,1)}, bf16[16,80,256]{2,1,0:T(8,128)(2,1)}, u32[]{:S(2)}, u32[]{:S(2)}) collective-permute-start(bf16[16,80,256]{2,1,0:T(8,128)(2,1)} %collective-permute-done.3.refs_1_), channel_id=1, source_target_pairs={{0,8},{8,0},{16,24},{24,16},{1,9},{9,1},{17,25},{25,17},{2,10},{10... | collective-permute-start | bytes 1966088 | tf_op jit(solution)/shard_map/ppermute | solution.py:360
  160.3 16.7 %copy-start.11 = (bf16[16,48,256]{2,1,0:T(8,128)(2,1)S(1)}, bf16[16,48,256]{2,1,0:T(8,128)(2,1)}, u32[]{:S(2)}) copy-start(bf16[16,48,256]{2,1,0:T(8,128)(2,1)} %copy-done.10) | copy-start | bytes 1179652
  160.3 32.2 %collective-permute-start.23 = (bf16[16,48,256]{2,1,0:T(8,128)(2,1)}, bf16[16,48,256]{2,1,0:T(8,128)(2,1)}, u32[]{:S(2)}, u32[]{:S(2)}) collective-permute-start(bf16[16,48,256]{2,1,0:T(8,128)(2,1)} %collective-permute-done.21.refs_1_), channel_id=1, source_target_pairs={{0,8},{8,0},{16,24},{24,16},{1,9},{9,1},{17,25},{25,17},{2,10},{10... | collective-permute-start | bytes 1179656 | tf_op jit(solution)/shard_map/ppermute | solution.py:360
  160.9 31.7 %collective-permute-start.26 = (bf16[16,48,256]{2,1,0:T(8,128)(2,1)}, bf16[16,48,256]{2,1,0:T(8,128)(2,1)}, u32[]{:S(2)}, u32[]{:S(2)}) collective-permute-start(bf16[16,48,256]{2,1,0:T(8,128)(2,1)} %collective-permute-done.24.refs_5_), channel_id=1, source_target_pairs={{0,8},{8,0},{16,24},{24,16},{1,9},{9,1},{17,25},{25,17},{2,10},{10... | collective-permute-start | bytes 1179656 | tf_op jit(solution)/shard_map/ppermute | solution.py:360
  176.4 30.8 %collective-permute-start.18 = (bf16[16,48,256]{2,1,0:T(8,128)(2,1)S(1)}, bf16[16,48,256]{2,1,0:T(8,128)(2,1)}, u32[]{:S(2)}, u32[]{:S(2)}) collective-permute-start(bf16[16,48,256]{2,1,0:T(8,128)(2,1)S(1)} %broadcast_select_fusion.1.refs_0_), channel_id=1, source_target_pairs={{0,8},{8,0},{16,24},{24,16},{1,9},{9,1},{17,25},{25,17},{2,10},{10... | collective-permute-start | bytes 1179656 | tf_op jit(solution)/shard_map/ppermute | solution.py:360
  176.9 30.3 %collective-permute-start.19 = (bf16[16,48,256]{2,1,0:T(8,128)(2,1)S(1)}, bf16[16,48,256]{2,1,0:T(8,128)(2,1)}, u32[]{:S(2)}, u32[]{:S(2)}) collective-permute-start(bf16[16,48,256]{2,1,0:T(8,128)(2,1)S(1)} %copy-done.11), channel_id=1, source_target_pairs={{0,8},{8,0},{16,24},{24,16},{1,9},{9,1},{17,25},{25,17},{2,10},{10... | collective-permute-start | bytes 1179656 | tf_op jit(solution)/shard_map/ppermute | solution.py:360
  190.9 48.2 %collective-permute-start.27 = (bf16[5120,128]{1,0:T(8,128)(2,1)}, bf16[5120,128]{1,0:T(8,128)(2,1)}, u32[]{:S(2)}, u32[]{:S(2)}) collective-permute-start(bf16[5120,128]{1,0:T(8,128)(2,1)} %get-tuple-element.19), channel_id=1, source_target_pairs={{0,1},{1,0},{2,3},{3,2},{4,5},{5,4},{6,7},{7,6},{8,9},{9,8},{10,11... | collective-permute-start | bytes 3932168 | tf_op jit(solution)/shard_map/ppermute | solution.py:360
  192.4 27.5 %collective-permute-start.30 = (bf16[1024,512]{1,0:T(8,128)(2,1)}, bf16[1024,512]{1,0:T(8,128)(2,1)}, u32[]{:S(2)}, u32[]{:S(2)}) collective-permute-start(bf16[1024,512]{1,0:T(8,128)(2,1)} %refs_4_.1), channel_id=1, source_target_pairs={{0,8},{8,0},{16,24},{24,16},{1,9},{9,1},{17,25},{25,17},{2,10},{10... | collective-permute-start | bytes 3145736 | tf_op jit(solution)/shard_map/ppermute | solution.py:360
  192.6 27.4 %collective-permute-start.31 = (bf16[1024,512]{1,0:T(8,128)(2,1)}, bf16[1024,512]{1,0:T(8,128)(2,1)}, u32[]{:S(2)}, u32[]{:S(2)}) collective-permute-start(bf16[1024,512]{1,0:T(8,128)(2,1)} %collective-permute-done.29.refs_5_), channel_id=1, source_target_pairs={{0,8},{8,0},{16,24},{24,16},{1,9},{9,1},{17,25},{25,17},{2,10},{10... | collective-permute-start | bytes 3145736 | tf_op jit(solution)/shard_map/ppermute | solution.py:360
  207.2 11.9 %copy-start.13 = (bf16[4,32,128]{2,1,0:T(8,128)(2,1)S(1)}, bf16[4,32,128]{2,1,0:T(8,128)(2,1)}, u32[]{:S(2)}) copy-start(bf16[4,32,128]{2,1,0:T(8,128)(2,1)} %param.8) | copy-start | bytes 98308
  218.5 20.6 %collective-permute-start.28 = (bf16[3072,128]{1,0:T(8,128)(2,1)}, bf16[3072,128]{1,0:T(8,128)(2,1)S(1)}, u32[]{:S(2)}, u32[]{:S(2)}) collective-permute-start(bf16[3072,128]{1,0:T(8,128)(2,1)} %get-tuple-element.20), channel_id=1, source_target_pairs={{0,1},{1,0},{2,3},{3,2},{4,5},{5,4},{6,7},{7,6},{8,9},{9,8},{10,11... | collective-permute-start | bytes 2359304 | tf_op jit(solution)/shard_map/ppermute | solution.py:360
  239.1 1.7 copy-start.1
  240.8 1.4 copy-start.3
where the time goes:
time: 256 us
  waiting for transfers between devices  128 us (50%)
  Pallas kernels  83 us (32%)
  starting transfers between devices  31.1 us (12%)
  local copies, waits for them, and re-layouts  7.66 us (3%)
  other arithmetic  6.11 us (2%)
    ppermute x32, waiting for transfers between devices, swap(): return lax.ppermute(value, axis, pairs)  128 us
    pallas_call x5, Pallas kernels, pool_blocks(): pl.pallas_call(functools.partial(pool_kernel, first, blocks, pieces, size...  66.2 us
    ppermute x32, starting transfers between devices, swap(): return lax.ppermute(value, axis, pairs)  31.1 us
    pallas_call x1, Pallas kernels, make_scores(): pl.pallas_call(functools.partial(score_kernel, masks, width ** (-0.5)), o...  13.5 us
    unnamed x30, local copies, waits for them, and re-layouts  5.58 us
  transfers between devices with their start and end apart: 32, of which 8 were waited for; matrix products, arithmetic and copies ran while one was open for 3% of the time, Pallas kernels for 26%

commit v1 on v0

--- a/solution.py
+++ b/solution.py
@@ -109,7 +109,7 @@
     return jnp.concatenate([field.astype(jnp.bfloat16) for field in fields], axis=0)
 
 
-def pool_kernel(first, blocks, pieces, size, unroll, earlier, own, places, *refs):
+def pool_kernel(first, distances, pieces, size, unroll, earlier, own, places, *refs):
     sources = refs[: len(pieces)]
     bags_refs = refs[len(pieces) : len(pieces) + 2]
     refs = refs[len(pieces) + 2 :]
@@ -124,18 +124,18 @@
         (pooled_ref,) = refs[:1]
         tables_ref, bags, low_ref, high_ref, sems = refs[1:]
         part = pooled_ref.shape[0]
-    count = tables_ref.shape[0]
+    count, blocks = tables_ref.shape[0], len(distances)
     tab_dev = count // blocks
     rows = tables_ref.shape[1 if own else 2]
     samples = bags.shape[3]
     stride = count + PAD
     halves = (low_ref, high_ref)
-    member = places[blocks]
+    member = places[1] * (0 if own else 1)
 
     soon, later = [], []
     for number, source in enumerate(bags_refs):
         for block in range(blocks):
-            rows_from = source.at[pl.ds(places[block] * tab_dev, tab_dev)]
+            rows_from = source.at[pl.ds((places[0] ^ distances[block]) * tab_dev, tab_dev)]
             target = bags.at[number, pl.ds(block * tab_dev, tab_dev)]
             copy = pltpu.make_async_copy(rows_from, target, sems.at[number * blocks + block])
             (later if block else soon).append(copy)
@@ -219,9 +219,11 @@
     theirs_ref[...] = sum_ref[...].astype(theirs_ref.dtype)
 
 
-def pool_blocks(places, sources, pieces, bags, tab_dev, part, first=0, earlier=(), project=None):
-    own = project is None and sources[0].shape[0] == tab_dev
-    blocks = places.shape[0] - 1
+def pool_blocks(
+    places, distances, sources, pieces, bags, tab_dev, part, first=0, earlier=(), project=None
+):
+    own = distances == [0]
+    blocks = len(distances)
     count = blocks * tab_dev
     size = sources[0].shape[0]
     rows = sources[0].shape[1 if own else 2]
@@ -248,7 +250,7 @@
         out_specs, more, specs = VMEM, (), []
     unroll = min(16, size)
     return pl.pallas_call(
-        functools.partial(pool_kernel, first, blocks, pieces, size, unroll, len(earlier), own),
+        functools.partial(pool_kernel, first, distances, pieces, size, unroll, len(earlier), own),
         out_shape=out_shape,
         in_specs=[SMEM] + [ANY] * (len(sources) + 2 + len(earlier)) + specs,
         out_specs=out_specs,
@@ -278,8 +280,8 @@
         copy.start()
 
     def compress(step, carry):
-        for inner in range(4):
-            k = step * 4 + inner
+        for inner in range(8):
+            k = step * 8 + inner
             columns = []
             for mine, theirs in zip(own, back):
                 part = mine.shape[0] // outs
@@ -290,11 +292,11 @@
             turned[pl.ds(k, samples, stride=step_k), :] = value
         return carry
 
-    lax.fori_loop(0, outs // 4, compress, 0)
+    lax.fori_loop(0, outs // 8, compress, 0)
 
     def interact(step, carry):
-        for inner in range(4):
-            b = step * 4 + inner
+        for inner in range(16):
+            b = step * 16 + inner
             value = turned[pl.ds(pl.multiple_of(b * step_k, PAD), outs), :].astype(jnp.bfloat16)
             zero = jnp.zeros_like(value)
             left = jnp.concatenate([value[:half], value[half:]], axis=1)
@@ -308,7 +310,7 @@
             inter[pl.ds(b, half, stride=step_b), :] = pairs * scale
         return carry
 
-    lax.fori_loop(0, samples // 4, interact, 0)
+    lax.fori_loop(0, samples // 16, interact, 0)
     for copy in copies:
         copy.wait()
     scores_ref[...] = jnp.zeros_like(scores_ref)
@@ -422,25 +424,34 @@
     order = position ^ jnp.arange(line)
     mixing = jnp.take(mixing, order, axis=1).reshape(outs, line * tab_dev)
 
-    where = jnp.stack([position, member * 0])
-    near = pool_blocks(where, [tables], [(0, 0)], bags, tab_dev, width)
+    mixing, where = lax.optimization_barrier((mixing, jnp.stack([position, member])))
+    near = pool_blocks(where, [0], [tables], [(0, 0)], bags, tab_dev, width)
     own, back = [], []
-    for (first, part), send in zip(cuts, sends):
+    for chunk, ((first, part), send) in enumerate(zip(cuts, sends)):
         slots, sources, pieces = [], [], []
         for distance in range(1, line):
             slots.append(line_slot(send, slots, distance, line, position))
             shared, masks = share(slots[-1], grp)
             sources.append(shared)
             pieces.append([(0 if distance == line - 1 else distance - 1, mask) for mask in masks])
-        pooled = [near]
-        if line > 2:
-            where = jnp.concatenate([order[1 : line - 1], member[None]]).astype(jnp.int32)
-            pooled.append(
-                pool_blocks(where, sum(sources[:-1], []), sum(pieces[:-1], []), bags, tab_dev, part)
-            )
-        where = jnp.stack([order[line - 1], member]).astype(jnp.int32)
+        pooled, groups = [near], [[distance] for distance in range(1, line - 1)]
+        if chunk == len(cuts) - 1:
+            groups = [sum(groups, [])] if groups else []
+        for group in groups:
+            arrays = sum([sources[distance - 1] for distance in group], [])
+            marks = [(group.index(d), mask) for d in group for _, mask in pieces[d - 1]]
+            pooled.append(pool_blocks(where, group, arrays, marks, bags, tab_dev, part))
         mine_sum, their_sum = pool_blocks(
-            where, sources[-1], pieces[-1], bags, tab_dev, part, first, tuple(pooled), mixing
+            where,
+            [line - 1],
+            sources[-1],
+            pieces[-1],
+            bags,
+            tab_dev,
+            part,
+            first,
+            tuple(pooled),
+            mixing,
         )
         own.append(mine_sum)
         back.append(swap(their_sum, "emb", emb, 1))

time: 256 us -> 264 us (1.031)
  starting transfers between devices: 31.1 us -> 53 us
  waiting for transfers between devices: 128 us -> 117 us
  other arithmetic: 6.11 us -> 3.11 us
    ppermute x32, starting transfers between devices: 31.1 us -> 53 us  [swap(): return lax.ppermute(value, axis, pairs)]
    ppermute x32, waiting for transfers between devices: 128 us -> 117 us  [swap(): return lax.ppermute(value, axis, pairs)]
    pallas_call x1, Pallas kernels: 13.5 us -> 10.2 us  [make_scores(): pl.pallas_call(functools.partial(score_kernel, masks, width ** (-0.5)), o...]
    pallas_call x5 -> x6, Pallas kernels: 66.2 us -> 68.6 us  [pool_blocks(): pl.pallas_call(functools.partial(pool_kernel, first, distances, pieces, s...]
  transfers between devices with their start and end apart: 32 -> 32, of which waited for: 8 -> 9; matrix products, arithmetic and copies ran while one was open for 3% -> 2% of each run, Pallas kernels for 26% -> 26%
where the time goes in v1:
time: 264 us; the launch traced here: 263 us
  waiting for transfers between devices  117 us (44%)
  Pallas kernels  82 us (31%)
  starting transfers between devices  53 us (20%)
  local copies, waits for them, and re-layouts  7.7 us (3%)
  other arithmetic  3.11 us (1%)
    ppermute x32, waiting for transfers between devices, swap(): return lax.ppermute(value, axis, pairs)  117 us
    pallas_call x6, Pallas kernels, pool_blocks(): pl.pallas_call(functools.partial(pool_kernel, first, distances, pieces, s...  68.6 us
    ppermute x32, starting transfers between devices, swap(): return lax.ppermute(value, axis, pairs)  53 us
    pallas_call x1, Pallas kernels, make_scores(): pl.pallas_call(functools.partial(score_kernel, masks, width ** (-0.5)), o...  10.2 us
    unnamed x30, local copies, waits for them, and re-layouts  6.35 us
  transfers between devices with their start and end apart: 32, of which 9 were waited for; matrix products, arithmetic and copies ran while one was open for 2% of the time, Pallas kernels for 26%

profile of v1, /device:TPU:0, one launch (start us, length us, event | category | flops | bytes accessed | tf_op | source)
XLA Modules:
  0.0 263.2 jit_solution(15052500194882827393)
XLA Ops:
  0.0 2.6 turn.1
  2.6 0.7 collective-permute-start.14
  3.3 5.8 %collective-permute-start.15 = (bf16[16,48,256]{2,1,0:T(8,128)(2,1)}, bf16[16,48,256]{2,1,0:T(8,128)(2,1)}, u32[]{:S(2)}, u32[]{:S(2)}) collective-permute-start(bf16[16,48,256]{2,1,0:T(8,128)(2,1)} %get-tuple-element.21), channel_id=1, source_target_pairs={{0,4},{1,5},{2,6},{3,7},{4,0},{5,1},{6,2},{7,3},{8,12},{9,13},{10,... | collective-permute-start | bytes 1179656 | tf_op jit(solution)/shard_map/ppermute | solution.py:362
  9.1 1.6 copy-done.2
  10.7 0.7 bags.1
  11.4 0.8 copy-done
  12.2 1.5 collective-permute-start.6
  13.8 0.7 collective-permute-start
  14.5 27.7 %collective-permute-start.20 = (bf16[16,48,256]{2,1,0:T(8,128)(2,1)S(1)}, bf16[16,48,256]{2,1,0:T(8,128)(2,1)}, u32[]{:S(2)}, u32[]{:S(2)}) collective-permute-start(bf16[16,48,256]{2,1,0:T(8,128)(2,1)S(1)} %copy-done.14), channel_id=1, source_target_pairs={{0,2},{1,3},{2,0},{3,1},{4,6},{5,7},{6,4},{7,5},{8,10},{9,11},{10,... | collective-permute-start | bytes 1179656 | tf_op jit(solution)/shard_map/ppermute | solution.py:362
  42.2 8.1 %collective-permute-done.15.refs_4_ = bf16[16,48,256]{2,1,0:T(8,128)(2,1)} collective-permute-done((bf16[16,48,256]{2,1,0:T(8,128)(2,1)}, bf16[16,48,256]{2,1,0:T(8,128)(2,1)}, u32[]{:S(2)}, u32[]{:S(2)}) %collective-permute-start.15) | collective-permute-done | bytes 393248 | tf_op jit(solution)/shard_map/ppermute | solution.py:362
  50.3 14.0 %collective-permute-done.1.refs_0_ = bf16[16,80,256]{2,1,0:T(8,128)(2,1)} collective-permute-done((bf16[16,80,256]{2,1,0:T(8,128)(2,1)}, bf16[16,80,256]{2,1,0:T(8,128)(2,1)}, u32[]{:S(2)}, u32[]{:S(2)}) %collective-permute-start.1) | collective-permute-done | bytes 655392 | tf_op jit(solution)/shard_map/ppermute | solution.py:362
  64.2 1.3 collective-permute-start.2
  65.5 6.1 %collective-permute-done.20.refs_0_ = bf16[16,48,256]{2,1,0:T(8,128)(2,1)} collective-permute-done((bf16[16,48,256]{2,1,0:T(8,128)(2,1)S(1)}, bf16[16,48,256]{2,1,0:T(8,128)(2,1)}, u32[]{:S(2)}, u32[]{:S(2)}) %collective-permute-start.20) | collective-permute-done | bytes 393248 | tf_op jit(solution)/shard_map/ppermute | solution.py:362
  71.6 1.3 collective-permute-start.16
  72.9 1.6 collective-permute-start.21
  74.5 11.2 %collective-permute-done.7.refs_0_ = bf16[16,80,256]{2,1,0:T(8,128)(2,1)} collective-permute-done((bf16[16,80,256]{2,1,0:T(8,128)(2,1)S(1)}, bf16[16,80,256]{2,1,0:T(8,128)(2,1)}, u32[]{:S(2)}, u32[]{:S(2)}) %collective-permute-start.7) | collective-permute-done | bytes 655392 | tf_op jit(solution)/shard_map/ppermute | solution.py:362
  85.6 1.5 collective-permute-start.8
  87.4 20.2 %collective-permute-done.16 = bf16[16,48,256]{2,1,0:T(8,128)(2,1)S(1)} collective-permute-done((bf16[16,48,256]{2,1,0:T(8,128)(2,1)}, bf16[16,48,256]{2,1,0:T(8,128)(2,1)S(1)}, u32[]{:S(2)}, u32[]{:S(2)}) %collective-permute-start.16) | collective-permute-done | bytes 393248 | tf_op jit(solution)/shard_map/ppermute | solution.py:362
  107.5 1.5 collective-permute-start.24
  109.1 0.6 collective-permute-start.9
  109.7 0.5 collective-permute-start.11
  110.2 0.9 broadcast_select_fusion.refs_0_
  111.1 8.6 %collective-permute-done.24.refs_5_ = bf16[16,48,256]{2,1,0:T(8,128)(2,1)S(1)} collective-permute-done((bf16[16,48,256]{2,1,0:T(8,128)(2,1)}, bf16[16,48,256]{2,1,0:T(8,128)(2,1)S(1)}, u32[]{:S(2)}, u32[]{:S(2)}) %collective-permute-start.24) | collective-permute-done | bytes 393248 | tf_op jit(solution)/shard_map/ppermute | solution.py:362
  119.7 1.5 collective-permute-start.17
  121.2 0.5 collective-permute-start.3
  122.0 0.6 gather_fusion
  122.9 19.3 %collective-permute-done.17.refs_1_ = bf16[16,48,256]{2,1,0:T(8,128)(2,1)S(1)} collective-permute-done((bf16[16,48,256]{2,1,0:T(8,128)(2,1)S(1)}, bf16[16,48,256]{2,1,0:T(8,128)(2,1)S(1)}, u32[]{:S(2)}, u32[]{:S(2)}) %collective-permute-start.17) | collective-permute-done | bytes 393248 | tf_op jit(solution)/shard_map/ppermute | solution.py:362
  142.2 0.8 copy-done.7
  143.0 1.5 collective-permute-start.29
  144.5 0.5 collective-permute-start.13
  145.0 0.6 broadcast_select_fusion.2.refs_9_.refs_8_
  145.6 10.7 %collective-permute-done.3.refs_1_ = bf16[16,80,256]{2,1,0:T(8,128)(2,1)} collective-permute-done((bf16[16,80,256]{2,1,0:T(8,128)(2,1)}, bf16[16,80,256]{2,1,0:T(8,128)(2,1)}, u32[]{:S(2)}, u32[]{:S(2)}) %collective-permute-start.3) | collective-permute-done | bytes 655392 | tf_op jit(solution)/shard_map/ppermute | solution.py:362
  156.4 0.5 collective-permute-start.5
  156.9 0.6 pad_add_fusion.places
  157.5 11.4 %pool.4.refs_6_ = bf16[128,64,256]{2,1,0:T(8,128)(2,1)} custom-call(s32[2]{0:T(128)} %pad_add_fusion.places, bf16[64,256,128]{2,1,0:T(8,128)(2,1)} %refs_0_.1, s32[256,4,128]{2,1,0:T(4,128)} %bitcast.16, s32[256,4,128]{2,1,0:T(4,128)} %bitcast.23), custom_call_target="tpu_custom_call" | custom-call | flops 2000000000 | bytes 1048576 | tf_op jit(solution)/shard_map/pool/pallas_call | solution.py:252
  169.0 9.0 %pool.5.refs_7_ = bf16[80,64,256]{2,1,0:T(8,128)(2,1)} custom-call(s32[2]{0:T(128)} %pad_add_fusion.places, bf16[16,80,256]{2,1,0:T(8,128)(2,1)} %collective-permute-done.7.refs_0_, bf16[16,80,256]{2,1,0:T(8,128)(2,1)} %collective-permute-done.8.refs_1_, bf16[16,80,256]{2,1,0:T(8,128)(2,1)} %collective-permute-done.9.refs_2_, ...), custom_call_target="tpu_custom_call" | custom-call | flops 2000000000 | bytes 1048576 | tf_op jit(solution)/shard_map/pool/pallas_call | solution.py:252
  178.6 9.0 %pool.6.refs_8_ = bf16[80,64,256]{2,1,0:T(8,128)(2,1)} custom-call(s32[2]{0:T(128)} %pad_add_fusion.places, bf16[16,80,256]{2,1,0:T(8,128)(2,1)} %collective-permute-done.1.refs_0_, bf16[16,80,256]{2,1,0:T(8,128)(2,1)} %collective-permute-done.11.refs_1_, bf16[16,80,256]{2,1,0:T(8,128)(2,1)} %collective-permute-done.12.refs_2_, ...), custom_call_target="tpu_custom_call" | custom-call | flops 2000000000 | bytes 1048576 | tf_op jit(solution)/shard_map/pool/pallas_call | solution.py:252
  188.2 13.7 %project.2 = (f32[5120,128]{1,0:T(8,128)}, bf16[5120,128]{1,0:T(8,128)(2,1)}) custom-call(s32[2]{0:T(128)} %pad_add_fusion.places, bf16[16,80,256]{2,1,0:T(8,128)(2,1)} %broadcast_select_fusion.refs_0_, bf16[16,80,256]{2,1,0:T(8,128)(2,1)} %collective-permute-done.3.refs_1_, bf16[16,80,256]{2,1,0:T(8,128)(2,1)} %collective-permute-done.4.refs_2_, ...), custom_call_target="tpu_custom_call" | custom-call | flops 2000000000 | bytes 1048576 | tf_op jit(solution)/shard_map/project/pallas_call | solution.py:252
  202.0 1.6 collective-permute-start.27
  203.6 0.5 collective-permute-start.31
  204.1 14.1 %pool.7.refs_7_ = bf16[48,128,256]{2,1,0:T(8,128)(2,1)} custom-call(s32[2]{0:T(128)} %pad_add_fusion.places, bf16[16,48,256]{2,1,0:T(8,128)(2,1)} %collective-permute-done.20.refs_0_, bf16[16,48,256]{2,1,0:T(8,128)(2,1)} %collective-permute-done.21.refs_1_, bf16[16,48,256]{2,1,0:T(8,128)(2,1)} %collective-permute-done.22.refs_2_, ...), custom_call_target="tpu_custom_call" | custom-call | flops 2000000000 | bytes 1048576 | tf_op jit(solution)/shard_map/pool/pallas_call | solution.py:252
  218.2 11.3 %project.3 = (f32[3072,128]{1,0:T(8,128)}, bf16[3072,128]{1,0:T(8,128)(2,1)}) custom-call(s32[2]{0:T(128)} %pad_add_fusion.places, bf16[16,48,256]{2,1,0:T(8,128)(2,1)} %copy-done.6, bf16[16,48,256]{2,1,0:T(8,128)(2,1)} %copy-done.7, bf16[16,48,256]{2,1,0:T(8,128)(2,1)} %collective-permute-done.18.refs_2_, ...), custom_call_target="tpu_custom_call" | custom-call | flops 2000000000 | bytes 1048576 | tf_op jit(solution)/shard_map/project/pallas_call | solution.py:252
  229.5 0.6 collective-permute-start.28
  230.2 0.8 convert_reduce_fusion.lead_ref
  231.0 18.8 %collective-permute-done.28.refs_3_ = bf16[3072,128]{1,0:T(8,128)(2,1)S(1)} collective-permute-done((bf16[3072,128]{1,0:T(8,128)(2,1)}, bf16[3072,128]{1,0:T(8,128)(2,1)S(1)}, u32[]{:S(2)}, u32[]{:S(2)}) %collective-permute-start.28) | collective-permute-done | bytes 786464 | tf_op jit(solution)/shard_map/ppermute | solution.py:362
  249.9 1.7 copy-done.1
  251.6 1.4 copy-done.3
  253.0 10.2 %scores.1 = f32[128,512]{1,0:T(8,128)} custom-call(s32[1]{0:T(128)} %bitcast.member_ref, f32[64]{0:T(128)S(1)} %convert_reduce_fusion.lead_ref, f32[128,128]{1,0:T(8,128)S(1)} %bitcast.22, f32[5120,128]{1,0:T(8,128)S(1)} %copy-done.1, f32[3072,128]{1,0:T(8,128)S(1)} %copy-done.3, bf16[5120,128]{1,0:T(8,128)(2,1)} %collective-permute-done.27.refs_2_, ...), custom_call_target="tpu_custom_call" | custom-call | flops 4000000000 | bytes 1048576 | tf_op jit(solution)/shard_map/scores/pallas_call | solution.py:340
  (74 shorter events, 2.2 us)
Async XLA Ops:
  0.0 9.1 %copy-start.4 = (s32[4,32,512]{2,1,0:T(8,128)S(1)}, s32[4,32,512]{2,1,0:T(8,128)}, u32[]{:S(2)}) copy-start(s32[4,32,512]{2,1,0:T(8,128)} %lengths_ref.1) | copy-start | bytes 786436
  0.0 87.1 %copy-start.9 = (bf16[64,513]{1,0:T(8,128)(2,1)S(1)}, bf16[64,513]{1,0:T(8,128)(2,1)}, u32[]{:S(2)}) copy-start(bf16[64,513]{1,0:T(8,128)(2,1)} %param.10) | copy-start | bytes 196996
  2.6 11.9 %collective-permute-start.14 = (bf16[16,48,256]{2,1,0:T(8,128)(2,1)}, bf16[16,48,256]{2,1,0:T(8,128)(2,1)S(1)}, u32[]{:S(2)}, u32[]{:S(2)}) collective-permute-start(bf16[16,48,256]{2,1,0:T(8,128)(2,1)} %get-tuple-element.21), channel_id=1, source_target_pairs={{2,4},{3,5},{4,2},{5,3},{10,12},{11,13},{12,10},{13,11},{18,20},{1... | collective-permute-start | bytes 1179656 | tf_op jit(solution)/shard_map/ppermute | solution.py:362
  3.3 47.0 %collective-permute-start.15 = (bf16[16,48,256]{2,1,0:T(8,128)(2,1)}, bf16[16,48,256]{2,1,0:T(8,128)(2,1)}, u32[]{:S(2)}, u32[]{:S(2)}) collective-permute-start(bf16[16,48,256]{2,1,0:T(8,128)(2,1)} %get-tuple-element.21), channel_id=1, source_target_pairs={{0,4},{1,5},{2,6},{3,7},{4,0},{5,1},{6,2},{7,3},{8,12},{9,13},{10,... | collective-permute-start | bytes 1179656 | tf_op jit(solution)/shard_map/ppermute | solution.py:362
  9.1 55.2 %collective-permute-start.1 = (bf16[16,80,256]{2,1,0:T(8,128)(2,1)}, bf16[16,80,256]{2,1,0:T(8,128)(2,1)}, u32[]{:S(2)}, u32[]{:S(2)}) collective-permute-start(bf16[16,80,256]{2,1,0:T(8,128)(2,1)} %get-tuple-element.16), channel_id=1, source_target_pairs={{0,4},{1,5},{2,6},{3,7},{4,0},{5,1},{6,2},{7,3},{8,12},{9,13},{10,... | collective-permute-start | bytes 1966088 | tf_op jit(solution)/shard_map/ppermute | solution.py:362
  9.1 1.6 copy-start.2
  10.7 3.0 %copy-start.11 = (bf16[16,80,256]{2,1,0:T(8,128)(2,1)S(1)}, bf16[16,80,256]{2,1,0:T(8,128)(2,1)}, u32[]{:S(2)}) copy-start(bf16[16,80,256]{2,1,0:T(8,128)(2,1)} %get-tuple-element.16) | copy-start | bytes 1966084
  10.7 3.7 %copy-start.14 = (bf16[16,48,256]{2,1,0:T(8,128)(2,1)S(1)}, bf16[16,48,256]{2,1,0:T(8,128)(2,1)}, u32[]{:S(2)}) copy-start(bf16[16,48,256]{2,1,0:T(8,128)(2,1)} %get-tuple-element.21) | copy-start | bytes 1179652
  11.4 0.8 copy-start
  12.2 60.6 %collective-permute-start.6 = (s32[1024,128]{1,0:T(8,128)S(1)}, s32[1024,128]{1,0:T(8,128)S(1)}, u32[]{:S(2)}, u32[]{:S(2)}) collective-permute-start(s32[1024,128]{1,0:T(8,128)S(1)} %get-tuple-element.18), channel_id=1, source_target_pairs={{0,1},{1,0},{2,3},{3,2},{4,5},{5,4},{6,7},{7,6},{8,9},{9,8},{10,11... | collective-permute-start | bytes 1572872 | tf_op jit(solution)/shard_map/ppermute | solution.py:362
  13.8 60.7 %collective-permute-start = (bf16[16,80,256]{2,1,0:T(8,128)(2,1)S(1)}, bf16[16,80,256]{2,1,0:T(8,128)(2,1)S(1)}, u32[]{:S(2)}, u32[]{:S(2)}) collective-permute-start(bf16[16,80,256]{2,1,0:T(8,128)(2,1)S(1)} %copy-done.11), channel_id=1, source_target_pairs={{2,4},{3,5},{4,2},{5,3},{10,12},{11,13},{12,10},{13,11},{18,20},{1... | collective-permute-start | bytes 1966088 | tf_op jit(solution)/shard_map/ppermute | solution.py:362
  14.5 57.1 %collective-permute-start.20 = (bf16[16,48,256]{2,1,0:T(8,128)(2,1)S(1)}, bf16[16,48,256]{2,1,0:T(8,128)(2,1)}, u32[]{:S(2)}, u32[]{:S(2)}) collective-permute-start(bf16[16,48,256]{2,1,0:T(8,128)(2,1)S(1)} %copy-done.14), channel_id=1, source_target_pairs={{0,2},{1,3},{2,0},{3,1},{4,6},{5,7},{6,4},{7,5},{8,10},{9,11},{10,... | collective-permute-start | bytes 1179656 | tf_op jit(solution)/shard_map/ppermute | solution.py:362
  50.2 35.4 %collective-permute-start.7 = (bf16[16,80,256]{2,1,0:T(8,128)(2,1)S(1)}, bf16[16,80,256]{2,1,0:T(8,128)(2,1)}, u32[]{:S(2)}, u32[]{:S(2)}) collective-permute-start(bf16[16,80,256]{2,1,0:T(8,128)(2,1)S(1)} %copy-done.11), channel_id=1, source_target_pairs={{0,2},{1,3},{2,0},{3,1},{4,6},{5,7},{6,4},{7,5},{8,10},{9,11},{10,... | collective-permute-start | bytes 1966088 | tf_op jit(solution)/shard_map/ppermute | solution.py:362
  64.2 45.4 %collective-permute-start.2 = (bf16[16,80,256]{2,1,0:T(8,128)(2,1)}, bf16[16,80,256]{2,1,0:T(8,128)(2,1)S(1)}, u32[]{:S(2)}, u32[]{:S(2)}) collective-permute-start(bf16[16,80,256]{2,1,0:T(8,128)(2,1)} %collective-permute-done.1.refs_0_), channel_id=1, source_target_pairs={{2,0},{3,1},{4,6},{5,7},{10,8},{11,9},{12,14},{13,15},{18,16},{19,... | collective-permute-start | bytes 1966088 | tf_op jit(solution)/shard_map/ppermute | solution.py:362
  71.6 35.9 %collective-permute-start.16 = (bf16[16,48,256]{2,1,0:T(8,128)(2,1)}, bf16[16,48,256]{2,1,0:T(8,128)(2,1)S(1)}, u32[]{:S(2)}, u32[]{:S(2)}) collective-permute-start(bf16[16,48,256]{2,1,0:T(8,128)(2,1)} %collective-permute-done.15.refs_4_), channel_id=1, source_target_pairs={{2,0},{3,1},{4,6},{5,7},{10,8},{11,9},{12,14},{13,15},{18,16},{19,... | collective-permute-start | bytes 1179656 | tf_op jit(solution)/shard_map/ppermute | solution.py:362
  72.9 84.6 %copy-start.5 = (s32[1024,128]{1,0:T(8,128)}, s32[1024,128]{1,0:T(8,128)S(1)}, u32[]{:S(2)}) copy-start(s32[1024,128]{1,0:T(8,128)S(1)} %collective-permute-done.6) | copy-start | bytes 1572868
  72.9 36.1 %collective-permute-start.21 = (bf16[16,48,256]{2,1,0:T(8,128)(2,1)}, bf16[16,48,256]{2,1,0:T(8,128)(2,1)}, u32[]{:S(2)}, u32[]{:S(2)}) collective-permute-start(bf16[16,48,256]{2,1,0:T(8,128)(2,1)} %collective-permute-done.20.refs_0_), channel_id=1, source_target_pairs={{0,16},{8,24},{16,0},{24,8},{1,17},{9,25},{17,1},{25,9},{2,18},{10... | collective-permute-start | bytes 1179656 | tf_op jit(solution)/shard_map/ppermute | solution.py:362
  74.5 34.6 %collective-permute-start.22 = (bf16[16,48,256]{2,1,0:T(8,128)(2,1)}, bf16[16,48,256]{2,1,0:T(8,128)(2,1)}, u32[]{:S(2)}, u32[]{:S(2)}) collective-permute-start(bf16[16,48,256]{2,1,0:T(8,128)(2,1)} %collective-permute-done.20.refs_0_), channel_id=1, source_target_pairs={{0,8},{8,0},{16,24},{24,16},{1,9},{9,1},{17,25},{25,17},{2,10},{10... | collective-permute-start | bytes 1179656 | tf_op jit(solution)/shard_map/ppermute | solution.py:362
  85.6 36.1 %collective-permute-start.8 = (bf16[16,80,256]{2,1,0:T(8,128)(2,1)}, bf16[16,80,256]{2,1,0:T(8,128)(2,1)}, u32[]{:S(2)}, u32[]{:S(2)}) collective-permute-start(bf16[16,80,256]{2,1,0:T(8,128)(2,1)} %collective-permute-done.7.refs_0_), channel_id=1, source_target_pairs={{0,16},{8,24},{16,0},{24,8},{1,17},{9,25},{17,1},{25,9},{2,18},{10... | collective-permute-start | bytes 1966088 | tf_op jit(solution)/shard_map/ppermute | solution.py:362
  107.5 12.2 %collective-permute-start.24 = (bf16[16,48,256]{2,1,0:T(8,128)(2,1)}, bf16[16,48,256]{2,1,0:T(8,128)(2,1)S(1)}, u32[]{:S(2)}, u32[]{:S(2)}) collective-permute-start(bf16[16,48,256]{2,1,0:T(8,128)(2,1)} %collective-permute-done.15.refs_4_), channel_id=1, source_target_pairs={{0,16},{8,24},{16,0},{24,8},{1,17},{9,25},{17,1},{25,9},{2,18},{10... | collective-permute-start | bytes 1179656 | tf_op jit(solution)/shard_map/ppermute | solution.py:362
  109.0 12.2 %collective-permute-start.25 = (bf16[16,48,256]{2,1,0:T(8,128)(2,1)}, bf16[16,48,256]{2,1,0:T(8,128)(2,1)S(1)}, u32[]{:S(2)}, u32[]{:S(2)}) collective-permute-start(bf16[16,48,256]{2,1,0:T(8,128)(2,1)} %collective-permute-done.15.refs_4_), channel_id=1, source_target_pairs={{0,8},{8,0},{16,24},{24,16},{1,9},{9,1},{17,25},{25,17},{2,10},{10... | collective-permute-start | bytes 1179656 | tf_op jit(solution)/shard_map/ppermute | solution.py:362
  109.1 78.5 %copy-start.6 = (bf16[16,48,256]{2,1,0:T(8,128)(2,1)}, bf16[16,48,256]{2,1,0:T(8,128)(2,1)S(1)}, u32[]{:S(2)}) copy-start(bf16[16,48,256]{2,1,0:T(8,128)(2,1)S(1)} %broadcast_select_fusion.1.refs_0_) | copy-start | bytes 1179652
  109.1 35.4 %collective-permute-start.9 = (bf16[16,80,256]{2,1,0:T(8,128)(2,1)}, bf16[16,80,256]{2,1,0:T(8,128)(2,1)}, u32[]{:S(2)}, u32[]{:S(2)}) collective-permute-start(bf16[16,80,256]{2,1,0:T(8,128)(2,1)} %collective-permute-done.7.refs_0_), channel_id=1, source_target_pairs={{0,8},{8,0},{16,24},{24,16},{1,9},{9,1},{17,25},{25,17},{2,10},{10... | collective-permute-start | bytes 1966088 | tf_op jit(solution)/shard_map/ppermute | solution.py:362
  109.7 34.8 %collective-permute-start.11 = (bf16[16,80,256]{2,1,0:T(8,128)(2,1)}, bf16[16,80,256]{2,1,0:T(8,128)(2,1)}, u32[]{:S(2)}, u32[]{:S(2)}) collective-permute-start(bf16[16,80,256]{2,1,0:T(8,128)(2,1)} %collective-permute-done.1.refs_0_), channel_id=1, source_target_pairs={{0,16},{8,24},{16,0},{24,8},{1,17},{9,25},{17,1},{25,9},{2,18},{10... | collective-permute-start | bytes 1966088 | tf_op jit(solution)/shard_map/ppermute | solution.py:362
  119.7 2.2 copy-start.12
  119.7 22.5 %collective-permute-start.17 = (bf16[16,48,256]{2,1,0:T(8,128)(2,1)S(1)}, bf16[16,48,256]{2,1,0:T(8,128)(2,1)S(1)}, u32[]{:S(2)}, u32[]{:S(2)}) collective-permute-start(bf16[16,48,256]{2,1,0:T(8,128)(2,1)S(1)} %broadcast_select_fusion.1.refs_0_), channel_id=1, source_target_pairs={{0,16},{8,24},{16,0},{24,8},{1,17},{9,25},{17,1},{25,9},{2,18},{10... | collective-permute-start | bytes 1179656 | tf_op jit(solution)/shard_map/ppermute | solution.py:362
  121.2 0.7 copy-start.13
  121.2 35.1 %collective-permute-start.3 = (bf16[16,80,256]{2,1,0:T(8,128)(2,1)}, bf16[16,80,256]{2,1,0:T(8,128)(2,1)}, u32[]{:S(2)}, u32[]{:S(2)}) collective-permute-start(bf16[16,80,256]{2,1,0:T(8,128)(2,1)} %broadcast_select_fusion.refs_0_), channel_id=1, source_target_pairs={{0,16},{8,24},{16,0},{24,8},{1,17},{9,25},{17,1},{25,9},{2,18},{10... | collective-permute-start | bytes 1966088 | tf_op jit(solution)/shard_map/ppermute | solution.py:362
  121.8 34.6 %collective-permute-start.10 = (bf16[16,80,256]{2,1,0:T(8,128)(2,1)}, bf16[16,80,256]{2,1,0:T(8,128)(2,1)}, u32[]{:S(2)}, u32[]{:S(2)}) collective-permute-start(bf16[16,80,256]{2,1,0:T(8,128)(2,1)} %collective-permute-done.8.refs_1_), channel_id=1, source_target_pairs={{0,8},{8,0},{16,24},{24,16},{1,9},{9,1},{17,25},{25,17},{2,10},{10... | collective-permute-start | bytes 1966088 | tf_op jit(solution)/shard_map/ppermute | solution.py:362
  142.2 0.8 copy-start.7
  143.0 59.0 %collective-permute-start.29 = (bf16[1024,512]{1,0:T(8,128)(2,1)}, bf16[1024,512]{1,0:T(8,128)(2,1)}, u32[]{:S(2)}, u32[]{:S(2)}) collective-permute-start(bf16[1024,512]{1,0:T(8,128)(2,1)} %refs_4_.1), channel_id=1, source_target_pairs={{0,16},{8,24},{16,0},{24,8},{1,17},{9,25},{17,1},{25,9},{2,18},{10... | collective-permute-start | bytes 3145736 | tf_op jit(solution)/shard_map/ppermute | solution.py:362
  144.5 33.5 %collective-permute-start.12 = (bf16[16,80,256]{2,1,0:T(8,128)(2,1)}, bf16[16,80,256]{2,1,0:T(8,128)(2,1)}, u32[]{:S(2)}, u32[]{:S(2)}) collective-permute-start(bf16[16,80,256]{2,1,0:T(8,128)(2,1)} %collective-permute-done.1.refs_0_), channel_id=1, source_target_pairs={{0,8},{8,0},{16,24},{24,16},{1,9},{9,1},{17,25},{25,17},{2,10},{10... | collective-permute-start | bytes 1966088 | tf_op jit(solution)/shard_map/ppermute | solution.py:362
  144.5 33.6 %collective-permute-start.13 = (bf16[16,80,256]{2,1,0:T(8,128)(2,1)}, bf16[16,80,256]{2,1,0:T(8,128)(2,1)}, u32[]{:S(2)}, u32[]{:S(2)}) collective-permute-start(bf16[16,80,256]{2,1,0:T(8,128)(2,1)} %collective-permute-done.11.refs_1_), channel_id=1, source_target_pairs={{0,8},{8,0},{16,24},{24,16},{1,9},{9,1},{17,25},{25,17},{2,10},{10... | collective-permute-start | bytes 1966088 | tf_op jit(solution)/shard_map/ppermute | solution.py:362
  156.3 31.3 %collective-permute-start.4 = (bf16[16,80,256]{2,1,0:T(8,128)(2,1)}, bf16[16,80,256]{2,1,0:T(8,128)(2,1)}, u32[]{:S(2)}, u32[]{:S(2)}) collective-permute-start(bf16[16,80,256]{2,1,0:T(8,128)(2,1)} %broadcast_select_fusion.refs_0_), channel_id=1, source_target_pairs={{0,8},{8,0},{16,24},{24,16},{1,9},{9,1},{17,25},{25,17},{2,10},{10... | collective-permute-start | bytes 1966088 | tf_op jit(solution)/shard_map/ppermute | solution.py:362
  156.4 31.4 %collective-permute-start.5 = (bf16[16,80,256]{2,1,0:T(8,128)(2,1)}, bf16[16,80,256]{2,1,0:T(8,128)(2,1)}, u32[]{:S(2)}, u32[]{:S(2)}) collective-permute-start(bf16[16,80,256]{2,1,0:T(8,128)(2,1)} %collective-permute-done.3.refs_1_), channel_id=1, source_target_pairs={{0,8},{8,0},{16,24},{24,16},{1,9},{9,1},{17,25},{25,17},{2,10},{10... | collective-permute-start | bytes 1966088 | tf_op jit(solution)/shard_map/ppermute | solution.py:362
  178.0 9.8 %copy-start.8 = (bf16[16,48,256]{2,1,0:T(8,128)(2,1)S(1)}, bf16[16,48,256]{2,1,0:T(8,128)(2,1)}, u32[]{:S(2)}) copy-start(bf16[16,48,256]{2,1,0:T(8,128)(2,1)} %copy-done.7) | copy-start | bytes 1179652
  178.0 25.6 %collective-permute-start.23 = (bf16[16,48,256]{2,1,0:T(8,128)(2,1)}, bf16[16,48,256]{2,1,0:T(8,128)(2,1)}, u32[]{:S(2)}, u32[]{:S(2)}) collective-permute-start(bf16[16,48,256]{2,1,0:T(8,128)(2,1)} %collective-permute-done.21.refs_1_), channel_id=1, source_target_pairs={{0,8},{8,0},{16,24},{24,16},{1,9},{9,1},{17,25},{25,17},{2,10},{10... | collective-permute-start | bytes 1179656 | tf_op jit(solution)/shard_map/ppermute | solution.py:362
  178.1 25.5 %collective-permute-start.26 = (bf16[16,48,256]{2,1,0:T(8,128)(2,1)}, bf16[16,48,256]{2,1,0:T(8,128)(2,1)}, u32[]{:S(2)}, u32[]{:S(2)}) collective-permute-start(bf16[16,48,256]{2,1,0:T(8,128)(2,1)} %copy-done.12), channel_id=1, source_target_pairs={{0,8},{8,0},{16,24},{24,16},{1,9},{9,1},{17,25},{25,17},{2,10},{10... | collective-permute-start | bytes 1179656 | tf_op jit(solution)/shard_map/ppermute | solution.py:362
  187.6 30.6 %collective-permute-start.18 = (bf16[16,48,256]{2,1,0:T(8,128)(2,1)S(1)}, bf16[16,48,256]{2,1,0:T(8,128)(2,1)}, u32[]{:S(2)}, u32[]{:S(2)}) collective-permute-start(bf16[16,48,256]{2,1,0:T(8,128)(2,1)S(1)} %broadcast_select_fusion.1.refs_0_), channel_id=1, source_target_pairs={{0,8},{8,0},{16,24},{24,16},{1,9},{9,1},{17,25},{25,17},{2,10},{10... | collective-permute-start | bytes 1179656 | tf_op jit(solution)/shard_map/ppermute | solution.py:362
  187.8 30.4 %collective-permute-start.19 = (bf16[16,48,256]{2,1,0:T(8,128)(2,1)S(1)}, bf16[16,48,256]{2,1,0:T(8,128)(2,1)}, u32[]{:S(2)}, u32[]{:S(2)}) collective-permute-start(bf16[16,48,256]{2,1,0:T(8,128)(2,1)S(1)} %copy-done.8), channel_id=1, source_target_pairs={{0,8},{8,0},{16,24},{24,16},{1,9},{9,1},{17,25},{25,17},{2,10},{10... | collective-permute-start | bytes 1179656 | tf_op jit(solution)/shard_map/ppermute | solution.py:362
  202.0 47.9 %collective-permute-start.27 = (bf16[5120,128]{1,0:T(8,128)(2,1)}, bf16[5120,128]{1,0:T(8,128)(2,1)}, u32[]{:S(2)}, u32[]{:S(2)}) collective-permute-start(bf16[5120,128]{1,0:T(8,128)(2,1)} %get-tuple-element.23), channel_id=1, source_target_pairs={{0,1},{1,0},{2,3},{3,2},{4,5},{5,4},{6,7},{7,6},{8,9},{9,8},{10,11... | collective-permute-start | bytes 3932168 | tf_op jit(solution)/shard_map/ppermute | solution.py:362
  203.5 27.5 %collective-permute-start.30 = (bf16[1024,512]{1,0:T(8,128)(2,1)}, bf16[1024,512]{1,0:T(8,128)(2,1)}, u32[]{:S(2)}, u32[]{:S(2)}) collective-permute-start(bf16[1024,512]{1,0:T(8,128)(2,1)} %refs_4_.1), channel_id=1, source_target_pairs={{0,8},{8,0},{16,24},{24,16},{1,9},{9,1},{17,25},{25,17},{2,10},{10... | collective-permute-start | bytes 3145736 | tf_op jit(solution)/shard_map/ppermute | solution.py:362
  203.6 27.5 %collective-permute-start.31 = (bf16[1024,512]{1,0:T(8,128)(2,1)}, bf16[1024,512]{1,0:T(8,128)(2,1)}, u32[]{:S(2)}, u32[]{:S(2)}) collective-permute-start(bf16[1024,512]{1,0:T(8,128)(2,1)} %collective-permute-done.29.refs_5_), channel_id=1, source_target_pairs={{0,8},{8,0},{16,24},{24,16},{1,9},{9,1},{17,25},{25,17},{2,10},{10... | collective-permute-start | bytes 3145736 | tf_op jit(solution)/shard_map/ppermute | solution.py:362
  218.2 11.9 %copy-start.10 = (bf16[4,32,128]{2,1,0:T(8,128)(2,1)S(1)}, bf16[4,32,128]{2,1,0:T(8,128)(2,1)}, u32[]{:S(2)}) copy-start(bf16[4,32,128]{2,1,0:T(8,128)(2,1)} %param.8) | copy-start | bytes 98308
  229.5 20.3 %collective-permute-start.28 = (bf16[3072,128]{1,0:T(8,128)(2,1)}, bf16[3072,128]{1,0:T(8,128)(2,1)S(1)}, u32[]{:S(2)}, u32[]{:S(2)}) collective-permute-start(bf16[3072,128]{1,0:T(8,128)(2,1)} %get-tuple-element.24), channel_id=1, source_target_pairs={{0,1},{1,0},{2,3},{3,2},{4,5},{5,4},{6,7},{7,6},{8,9},{9,8},{10,11... | collective-permute-start | bytes 2359304 | tf_op jit(solution)/shard_map/ppermute | solution.py:362
  249.9 1.7 copy-start.1
  251.6 1.4 copy-start.3

commit v2 on v1

--- a/solution.py
+++ b/solution.py
@@ -187,15 +187,15 @@
     if not earlier:
 
         def narrow(step, carry):
-            for inner in range(4):
-                column = step * 4 + inner
+            for inner in range(16):
+                column = step * 16 + inner
                 start = pl.multiple_of(column * stride, PAD)
                 for half in range(2):
                     value = halves[half][pl.ds(start, count), :].astype(jnp.bfloat16)
                     pooled_ref[column, :, half * samples : (half + 1) * samples] = value
             return carry
 
-        lax.fori_loop(0, part // 4, narrow, 0)
+        lax.fori_loop(0, part // 16, narrow, 0)
         return
 
     outs = project_ref.shape[0]
@@ -203,8 +203,8 @@
         copy.wait()
 
     def some_columns(step, carry):
-        for inner in range(4):
-            column = step * 4 + inner
+        for inner in range(16):
+            column = step * 16 + inner
             start = pl.multiple_of(column * stride, PAD)
             here = [ref[pl.ds(start, count), :].astype(jnp.bfloat16) for ref in halves]
             pooled = jnp.concatenate(
@@ -215,7 +215,7 @@
             sum_ref[pl.ds(column, outs, stride=part), :] = total[:, samples:]
         return carry
 
-    lax.fori_loop(0, part // 4, some_columns, 0)
+    lax.fori_loop(0, part // 16, some_columns, 0)
     theirs_ref[...] = sum_ref[...].astype(theirs_ref.dtype)
 
 

time: 264 us -> 262 us (level)
  Pallas kernels: 82 us -> 79.2 us
    pallas_call x6, Pallas kernels: 68.6 us -> 65.8 us  [pool_blocks(): pl.pallas_call(functools.partial(pool_kernel, first, distances, pieces, s...]
  transfers between devices with their start and end apart: 32 -> 32, of which waited for: 9 -> 9; matrix products, arithmetic and copies ran while one was open for 2% -> 2% of each run, Pallas kernels for 26% -> 25%
where the time goes in v2:
time: 262 us
  waiting for transfers between devices  118 us (45%)
  Pallas kernels  79.2 us (30%)
  starting transfers between devices  53 us (20%)
  local copies, waits for them, and re-layouts  7.7 us (3%)
  other arithmetic  3.11 us (1%)
    ppermute x32, waiting for transfers between devices, swap(): return lax.ppermute(value, axis, pairs)  118 us
    pallas_call x6, Pallas kernels, pool_blocks(): pl.pallas_call(functools.partial(pool_kernel, first, distances, pieces, s...  65.8 us
    ppermute x32, starting transfers between devices, swap(): return lax.ppermute(value, axis, pairs)  53 us
    pallas_call x1, Pallas kernels, make_scores(): pl.pallas_call(functools.partial(score_kernel, masks, width ** (-0.5)), o...  10.2 us
    unnamed x30, local copies, waits for them, and re-layouts  6.35 us
  transfers between devices with their start and end apart: 32, of which 9 were waited for; matrix products, arithmetic and copies ran while one was open for 2% of the time, Pallas kernels for 25%

profile of v2, /device:TPU:0, one launch (start us, length us, event | category | flops | bytes accessed | tf_op | source)
XLA Modules:
  0.0 261.5 jit_solution(16207204070307336631)
XLA Ops:
  0.0 2.6 turn.1
  2.6 0.7 collective-permute-start.14
  3.3 5.8 %collective-permute-start.15 = (bf16[16,48,256]{2,1,0:T(8,128)(2,1)}, bf16[16,48,256]{2,1,0:T(8,128)(2,1)}, u32[]{:S(2)}, u32[]{:S(2)}) collective-permute-start(bf16[16,48,256]{2,1,0:T(8,128)(2,1)} %get-tuple-element.21), channel_id=1, source_target_pairs={{0,4},{1,5},{2,6},{3,7},{4,0},{5,1},{6,2},{7,3},{8,12},{9,13},{10,... | collective-permute-start | bytes 1179656 | tf_op jit(solution)/shard_map/ppermute | solution.py:362
  9.1 1.6 copy-done.2
  10.7 0.7 bags.1
  11.4 0.8 copy-done
  12.2 1.5 collective-permute-start.6
  13.8 0.7 collective-permute-start
  14.5 27.7 %collective-permute-start.20 = (bf16[16,48,256]{2,1,0:T(8,128)(2,1)S(1)}, bf16[16,48,256]{2,1,0:T(8,128)(2,1)}, u32[]{:S(2)}, u32[]{:S(2)}) collective-permute-start(bf16[16,48,256]{2,1,0:T(8,128)(2,1)S(1)} %copy-done.14), channel_id=1, source_target_pairs={{0,2},{1,3},{2,0},{3,1},{4,6},{5,7},{6,4},{7,5},{8,10},{9,11},{10,... | collective-permute-start | bytes 1179656 | tf_op jit(solution)/shard_map/ppermute | solution.py:362
  42.2 8.1 %collective-permute-done.15.refs_4_ = bf16[16,48,256]{2,1,0:T(8,128)(2,1)} collective-permute-done((bf16[16,48,256]{2,1,0:T(8,128)(2,1)}, bf16[16,48,256]{2,1,0:T(8,128)(2,1)}, u32[]{:S(2)}, u32[]{:S(2)}) %collective-permute-start.15) | collective-permute-done | bytes 393248 | tf_op jit(solution)/shard_map/ppermute | solution.py:362
  50.3 14.0 %collective-permute-done.1.refs_0_ = bf16[16,80,256]{2,1,0:T(8,128)(2,1)} collective-permute-done((bf16[16,80,256]{2,1,0:T(8,128)(2,1)}, bf16[16,80,256]{2,1,0:T(8,128)(2,1)}, u32[]{:S(2)}, u32[]{:S(2)}) %collective-permute-start.1) | collective-permute-done | bytes 655392 | tf_op jit(solution)/shard_map/ppermute | solution.py:362
  64.2 1.3 collective-permute-start.2
  65.5 6.1 %collective-permute-done.20.refs_0_ = bf16[16,48,256]{2,1,0:T(8,128)(2,1)} collective-permute-done((bf16[16,48,256]{2,1,0:T(8,128)(2,1)S(1)}, bf16[16,48,256]{2,1,0:T(8,128)(2,1)}, u32[]{:S(2)}, u32[]{:S(2)}) %collective-permute-start.20) | collective-permute-done | bytes 393248 | tf_op jit(solution)/shard_map/ppermute | solution.py:362
  71.6 1.3 collective-permute-start.16
  72.9 1.6 collective-permute-start.21
  74.5 11.2 %collective-permute-done.7.refs_0_ = bf16[16,80,256]{2,1,0:T(8,128)(2,1)} collective-permute-done((bf16[16,80,256]{2,1,0:T(8,128)(2,1)S(1)}, bf16[16,80,256]{2,1,0:T(8,128)(2,1)}, u32[]{:S(2)}, u32[]{:S(2)}) %collective-permute-start.7) | collective-permute-done | bytes 655392 | tf_op jit(solution)/shard_map/ppermute | solution.py:362
  85.6 1.5 collective-permute-start.8
  87.4 20.2 %collective-permute-done.16 = bf16[16,48,256]{2,1,0:T(8,128)(2,1)S(1)} collective-permute-done((bf16[16,48,256]{2,1,0:T(8,128)(2,1)}, bf16[16,48,256]{2,1,0:T(8,128)(2,1)S(1)}, u32[]{:S(2)}, u32[]{:S(2)}) %collective-permute-start.16) | collective-permute-done | bytes 393248 | tf_op jit(solution)/shard_map/ppermute | solution.py:362
  107.5 1.5 collective-permute-start.24
  109.1 0.6 collective-permute-start.9
  109.7 0.5 collective-permute-start.11
  110.2 0.9 broadcast_select_fusion.refs_0_
  111.1 8.6 %collective-permute-done.24.refs_5_ = bf16[16,48,256]{2,1,0:T(8,128)(2,1)S(1)} collective-permute-done((bf16[16,48,256]{2,1,0:T(8,128)(2,1)}, bf16[16,48,256]{2,1,0:T(8,128)(2,1)S(1)}, u32[]{:S(2)}, u32[]{:S(2)}) %collective-permute-start.24) | collective-permute-done | bytes 393248 | tf_op jit(solution)/shard_map/ppermute | solution.py:362
  119.7 1.5 collective-permute-start.17
  121.2 0.5 collective-permute-start.3
  122.0 0.6 gather_fusion
  122.9 19.3 %collective-permute-done.17.refs_1_ = bf16[16,48,256]{2,1,0:T(8,128)(2,1)S(1)} collective-permute-done((bf16[16,48,256]{2,1,0:T(8,128)(2,1)S(1)}, bf16[16,48,256]{2,1,0:T(8,128)(2,1)S(1)}, u32[]{:S(2)}, u32[]{:S(2)}) %collective-permute-start.17) | collective-permute-done | bytes 393248 | tf_op jit(solution)/shard_map/ppermute | solution.py:362
  142.2 0.8 copy-done.7
  143.0 1.5 collective-permute-start.29
  144.5 0.5 collective-permute-start.13
  145.0 0.6 broadcast_select_fusion.2.refs_9_.refs_8_
  145.6 10.7 %collective-permute-done.3.refs_1_ = bf16[16,80,256]{2,1,0:T(8,128)(2,1)} collective-permute-done((bf16[16,80,256]{2,1,0:T(8,128)(2,1)}, bf16[16,80,256]{2,1,0:T(8,128)(2,1)}, u32[]{:S(2)}, u32[]{:S(2)}) %collective-permute-start.3) | collective-permute-done | bytes 655392 | tf_op jit(solution)/shard_map/ppermute | solution.py:362
  156.4 0.5 collective-permute-start.5
  156.9 0.6 pad_add_fusion.places
  157.5 11.3 %pool.4.refs_6_ = bf16[128,64,256]{2,1,0:T(8,128)(2,1)} custom-call(s32[2]{0:T(128)} %pad_add_fusion.places, bf16[64,256,128]{2,1,0:T(8,128)(2,1)} %refs_0_.1, s32[256,4,128]{2,1,0:T(4,128)} %bitcast.16, s32[256,4,128]{2,1,0:T(4,128)} %bitcast.23), custom_call_target="tpu_custom_call" | custom-call | flops 2000000000 | bytes 1048576 | tf_op jit(solution)/shard_map/pool/pallas_call | solution.py:252
  168.8 8.9 %pool.5.refs_7_ = bf16[80,64,256]{2,1,0:T(8,128)(2,1)} custom-call(s32[2]{0:T(128)} %pad_add_fusion.places, bf16[16,80,256]{2,1,0:T(8,128)(2,1)} %collective-permute-done.7.refs_0_, bf16[16,80,256]{2,1,0:T(8,128)(2,1)} %collective-permute-done.8.refs_1_, bf16[16,80,256]{2,1,0:T(8,128)(2,1)} %collective-permute-done.9.refs_2_, ...), custom_call_target="tpu_custom_call" | custom-call | flops 2000000000 | bytes 1048576 | tf_op jit(solution)/shard_map/pool/pallas_call | solution.py:252
  178.4 9.0 %pool.6.refs_8_ = bf16[80,64,256]{2,1,0:T(8,128)(2,1)} custom-call(s32[2]{0:T(128)} %pad_add_fusion.places, bf16[16,80,256]{2,1,0:T(8,128)(2,1)} %collective-permute-done.1.refs_0_, bf16[16,80,256]{2,1,0:T(8,128)(2,1)} %collective-permute-done.11.refs_1_, bf16[16,80,256]{2,1,0:T(8,128)(2,1)} %collective-permute-done.12.refs_2_, ...), custom_call_target="tpu_custom_call" | custom-call | flops 2000000000 | bytes 1048576 | tf_op jit(solution)/shard_map/pool/pallas_call | solution.py:252
  188.0 12.2 %project.2 = (f32[5120,128]{1,0:T(8,128)}, bf16[5120,128]{1,0:T(8,128)(2,1)}) custom-call(s32[2]{0:T(128)} %pad_add_fusion.places, bf16[16,80,256]{2,1,0:T(8,128)(2,1)} %broadcast_select_fusion.refs_0_, bf16[16,80,256]{2,1,0:T(8,128)(2,1)} %collective-permute-done.3.refs_1_, bf16[16,80,256]{2,1,0:T(8,128)(2,1)} %collective-permute-done.4.refs_2_, ...), custom_call_target="tpu_custom_call" | custom-call | flops 2000000000 | bytes 1048576 | tf_op jit(solution)/shard_map/project/pallas_call | solution.py:252
  200.1 1.6 collective-permute-start.27
  201.7 0.5 collective-permute-start.31
  202.2 14.1 %pool.7.refs_7_ = bf16[48,128,256]{2,1,0:T(8,128)(2,1)} custom-call(s32[2]{0:T(128)} %pad_add_fusion.places, bf16[16,48,256]{2,1,0:T(8,128)(2,1)} %collective-permute-done.20.refs_0_, bf16[16,48,256]{2,1,0:T(8,128)(2,1)} %collective-permute-done.21.refs_1_, bf16[16,48,256]{2,1,0:T(8,128)(2,1)} %collective-permute-done.22.refs_2_, ...), custom_call_target="tpu_custom_call" | custom-call | flops 2000000000 | bytes 1048576 | tf_op jit(solution)/shard_map/pool/pallas_call | solution.py:252
  216.4 10.3 %project.3 = (f32[3072,128]{1,0:T(8,128)}, bf16[3072,128]{1,0:T(8,128)(2,1)}) custom-call(s32[2]{0:T(128)} %pad_add_fusion.places, bf16[16,48,256]{2,1,0:T(8,128)(2,1)} %copy-done.6, bf16[16,48,256]{2,1,0:T(8,128)(2,1)} %copy-done.7, bf16[16,48,256]{2,1,0:T(8,128)(2,1)} %collective-permute-done.18.refs_2_, ...), custom_call_target="tpu_custom_call" | custom-call | flops 2000000000 | bytes 1048576 | tf_op jit(solution)/shard_map/project/pallas_call | solution.py:252
  226.7 0.6 collective-permute-start.28
  227.4 0.8 convert_reduce_fusion.lead_ref
  228.2 19.8 %collective-permute-done.28.refs_3_ = bf16[3072,128]{1,0:T(8,128)(2,1)S(1)} collective-permute-done((bf16[3072,128]{1,0:T(8,128)(2,1)}, bf16[3072,128]{1,0:T(8,128)(2,1)S(1)}, u32[]{:S(2)}, u32[]{:S(2)}) %collective-permute-start.28) | collective-permute-done | bytes 786464 | tf_op jit(solution)/shard_map/ppermute | solution.py:362
  248.0 1.7 copy-done.1
  249.8 1.4 copy-done.3
  251.2 10.2 %scores.1 = f32[128,512]{1,0:T(8,128)} custom-call(s32[1]{0:T(128)} %bitcast.member_ref, f32[64]{0:T(128)S(1)} %convert_reduce_fusion.lead_ref, f32[128,128]{1,0:T(8,128)S(1)} %bitcast.22, f32[5120,128]{1,0:T(8,128)S(1)} %copy-done.1, f32[3072,128]{1,0:T(8,128)S(1)} %copy-done.3, bf16[5120,128]{1,0:T(8,128)(2,1)} %collective-permute-done.27.refs_2_, ...), custom_call_target="tpu_custom_call" | custom-call | flops 4000000000 | bytes 1048576 | tf_op jit(solution)/shard_map/scores/pallas_call | solution.py:340
  (74 shorter events, 2.2 us)
Async XLA Ops:
  0.0 9.1 %copy-start.4 = (s32[4,32,512]{2,1,0:T(8,128)S(1)}, s32[4,32,512]{2,1,0:T(8,128)}, u32[]{:S(2)}) copy-start(s32[4,32,512]{2,1,0:T(8,128)} %lengths_ref.1) | copy-start | bytes 786436
  0.0 87.1 %copy-start.9 = (bf16[64,513]{1,0:T(8,128)(2,1)S(1)}, bf16[64,513]{1,0:T(8,128)(2,1)}, u32[]{:S(2)}) copy-start(bf16[64,513]{1,0:T(8,128)(2,1)} %param.10) | copy-start | bytes 196996
  2.6 11.9 %collective-permute-start.14 = (bf16[16,48,256]{2,1,0:T(8,128)(2,1)}, bf16[16,48,256]{2,1,0:T(8,128)(2,1)S(1)}, u32[]{:S(2)}, u32[]{:S(2)}) collective-permute-start(bf16[16,48,256]{2,1,0:T(8,128)(2,1)} %get-tuple-element.21), channel_id=1, source_target_pairs={{2,4},{3,5},{4,2},{5,3},{10,12},{11,13},{12,10},{13,11},{18,20},{1... | collective-permute-start | bytes 1179656 | tf_op jit(solution)/shard_map/ppermute | solution.py:362
  3.3 47.0 %collective-permute-start.15 = (bf16[16,48,256]{2,1,0:T(8,128)(2,1)}, bf16[16,48,256]{2,1,0:T(8,128)(2,1)}, u32[]{:S(2)}, u32[]{:S(2)}) collective-permute-start(bf16[16,48,256]{2,1,0:T(8,128)(2,1)} %get-tuple-element.21), channel_id=1, source_target_pairs={{0,4},{1,5},{2,6},{3,7},{4,0},{5,1},{6,2},{7,3},{8,12},{9,13},{10,... | collective-permute-start | bytes 1179656 | tf_op jit(solution)/shard_map/ppermute | solution.py:362
  9.1 55.2 %collective-permute-start.1 = (bf16[16,80,256]{2,1,0:T(8,128)(2,1)}, bf16[16,80,256]{2,1,0:T(8,128)(2,1)}, u32[]{:S(2)}, u32[]{:S(2)}) collective-permute-start(bf16[16,80,256]{2,1,0:T(8,128)(2,1)} %get-tuple-element.16), channel_id=1, source_target_pairs={{0,4},{1,5},{2,6},{3,7},{4,0},{5,1},{6,2},{7,3},{8,12},{9,13},{10,... | collective-permute-start | bytes 1966088 | tf_op jit(solution)/shard_map/ppermute | solution.py:362
  9.1 1.6 copy-start.2
  10.7 3.0 %copy-start.11 = (bf16[16,80,256]{2,1,0:T(8,128)(2,1)S(1)}, bf16[16,80,256]{2,1,0:T(8,128)(2,1)}, u32[]{:S(2)}) copy-start(bf16[16,80,256]{2,1,0:T(8,128)(2,1)} %get-tuple-element.16) | copy-start | bytes 1966084
  10.7 3.7 %copy-start.14 = (bf16[16,48,256]{2,1,0:T(8,128)(2,1)S(1)}, bf16[16,48,256]{2,1,0:T(8,128)(2,1)}, u32[]{:S(2)}) copy-start(bf16[16,48,256]{2,1,0:T(8,128)(2,1)} %get-tuple-element.21) | copy-start | bytes 1179652
  11.4 0.8 copy-start
  12.2 60.6 %collective-permute-start.6 = (s32[1024,128]{1,0:T(8,128)S(1)}, s32[1024,128]{1,0:T(8,128)S(1)}, u32[]{:S(2)}, u32[]{:S(2)}) collective-permute-start(s32[1024,128]{1,0:T(8,128)S(1)} %get-tuple-element.18), channel_id=1, source_target_pairs={{0,1},{1,0},{2,3},{3,2},{4,5},{5,4},{6,7},{7,6},{8,9},{9,8},{10,11... | collective-permute-start | bytes 1572872 | tf_op jit(solution)/shard_map/ppermute | solution.py:362
  13.8 60.7 %collective-permute-start = (bf16[16,80,256]{2,1,0:T(8,128)(2,1)S(1)}, bf16[16,80,256]{2,1,0:T(8,128)(2,1)S(1)}, u32[]{:S(2)}, u32[]{:S(2)}) collective-permute-start(bf16[16,80,256]{2,1,0:T(8,128)(2,1)S(1)} %copy-done.11), channel_id=1, source_target_pairs={{2,4},{3,5},{4,2},{5,3},{10,12},{11,13},{12,10},{13,11},{18,20},{1... | collective-permute-start | bytes 1966088 | tf_op jit(solution)/shard_map/ppermute | solution.py:362
  14.5 57.1 %collective-permute-start.20 = (bf16[16,48,256]{2,1,0:T(8,128)(2,1)S(1)}, bf16[16,48,256]{2,1,0:T(8,128)(2,1)}, u32[]{:S(2)}, u32[]{:S(2)}) collective-permute-start(bf16[16,48,256]{2,1,0:T(8,128)(2,1)S(1)} %copy-done.14), channel_id=1, source_target_pairs={{0,2},{1,3},{2,0},{3,1},{4,6},{5,7},{6,4},{7,5},{8,10},{9,11},{10,... | collective-permute-start | bytes 1179656 | tf_op jit(solution)/shard_map/ppermute | solution.py:362
  50.2 35.4 %collective-permute-start.7 = (bf16[16,80,256]{2,1,0:T(8,128)(2,1)S(1)}, bf16[16,80,256]{2,1,0:T(8,128)(2,1)}, u32[]{:S(2)}, u32[]{:S(2)}) collective-permute-start(bf16[16,80,256]{2,1,0:T(8,128)(2,1)S(1)} %copy-done.11), channel_id=1, source_target_pairs={{0,2},{1,3},{2,0},{3,1},{4,6},{5,7},{6,4},{7,5},{8,10},{9,11},{10,... | collective-permute-start | bytes 1966088 | tf_op jit(solution)/shard_map/ppermute | solution.py:362
  64.2 45.4 %collective-permute-start.2 = (bf16[16,80,256]{2,1,0:T(8,128)(2,1)}, bf16[16,80,256]{2,1,0:T(8,128)(2,1)S(1)}, u32[]{:S(2)}, u32[]{:S(2)}) collective-permute-start(bf16[16,80,256]{2,1,0:T(8,128)(2,1)} %collective-permute-done.1.refs_0_), channel_id=1, source_target_pairs={{2,0},{3,1},{4,6},{5,7},{10,8},{11,9},{12,14},{13,15},{18,16},{19,... | collective-permute-start | bytes 1966088 | tf_op jit(solution)/shard_map/ppermute | solution.py:362
  71.6 35.9 %collective-permute-start.16 = (bf16[16,48,256]{2,1,0:T(8,128)(2,1)}, bf16[16,48,256]{2,1,0:T(8,128)(2,1)S(1)}, u32[]{:S(2)}, u32[]{:S(2)}) collective-permute-start(bf16[16,48,256]{2,1,0:T(8,128)(2,1)} %collective-permute-done.15.refs_4_), channel_id=1, source_target_pairs={{2,0},{3,1},{4,6},{5,7},{10,8},{11,9},{12,14},{13,15},{18,16},{19,... | collective-permute-start | bytes 1179656 | tf_op jit(solution)/shard_map/ppermute | solution.py:362
  72.9 84.6 %copy-start.5 = (s32[1024,128]{1,0:T(8,128)}, s32[1024,128]{1,0:T(8,128)S(1)}, u32[]{:S(2)}) copy-start(s32[1024,128]{1,0:T(8,128)S(1)} %collective-permute-done.6) | copy-start | bytes 1572868
  72.9 36.1 %collective-permute-start.21 = (bf16[16,48,256]{2,1,0:T(8,128)(2,1)}, bf16[16,48,256]{2,1,0:T(8,128)(2,1)}, u32[]{:S(2)}, u32[]{:S(2)}) collective-permute-start(bf16[16,48,256]{2,1,0:T(8,128)(2,1)} %collective-permute-done.20.refs_0_), channel_id=1, source_target_pairs={{0,16},{8,24},{16,0},{24,8},{1,17},{9,25},{17,1},{25,9},{2,18},{10... | collective-permute-start | bytes 1179656 | tf_op jit(solution)/shard_map/ppermute | solution.py:362
  74.5 34.6 %collective-permute-start.22 = (bf16[16,48,256]{2,1,0:T(8,128)(2,1)}, bf16[16,48,256]{2,1,0:T(8,128)(2,1)}, u32[]{:S(2)}, u32[]{:S(2)}) collective-permute-start(bf16[16,48,256]{2,1,0:T(8,128)(2,1)} %collective-permute-done.20.refs_0_), channel_id=1, source_target_pairs={{0,8},{8,0},{16,24},{24,16},{1,9},{9,1},{17,25},{25,17},{2,10},{10... | collective-permute-start | bytes 1179656 | tf_op jit(solution)/shard_map/ppermute | solution.py:362
  85.6 36.1 %collective-permute-start.8 = (bf16[16,80,256]{2,1,0:T(8,128)(2,1)}, bf16[16,80,256]{2,1,0:T(8,128)(2,1)}, u32[]{:S(2)}, u32[]{:S(2)}) collective-permute-start(bf16[16,80,256]{2,1,0:T(8,128)(2,1)} %collective-permute-done.7.refs_0_), channel_id=1, source_target_pairs={{0,16},{8,24},{16,0},{24,8},{1,17},{9,25},{17,1},{25,9},{2,18},{10... | collective-permute-start | bytes 1966088 | tf_op jit(solution)/shard_map/ppermute | solution.py:362
  107.5 12.2 %collective-permute-start.24 = (bf16[16,48,256]{2,1,0:T(8,128)(2,1)}, bf16[16,48,256]{2,1,0:T(8,128)(2,1)S(1)}, u32[]{:S(2)}, u32[]{:S(2)}) collective-permute-start(bf16[16,48,256]{2,1,0:T(8,128)(2,1)} %collective-permute-done.15.refs_4_), channel_id=1, source_target_pairs={{0,16},{8,24},{16,0},{24,8},{1,17},{9,25},{17,1},{25,9},{2,18},{10... | collective-permute-start | bytes 1179656 | tf_op jit(solution)/shard_map/ppermute | solution.py:362
  109.0 12.2 %collective-permute-start.25 = (bf16[16,48,256]{2,1,0:T(8,128)(2,1)}, bf16[16,48,256]{2,1,0:T(8,128)(2,1)S(1)}, u32[]{:S(2)}, u32[]{:S(2)}) collective-permute-start(bf16[16,48,256]{2,1,0:T(8,128)(2,1)} %collective-permute-done.15.refs_4_), channel_id=1, source_target_pairs={{0,8},{8,0},{16,24},{24,16},{1,9},{9,1},{17,25},{25,17},{2,10},{10... | collective-permute-start | bytes 1179656 | tf_op jit(solution)/shard_map/ppermute | solution.py:362
  109.1 78.3 %copy-start.6 = (bf16[16,48,256]{2,1,0:T(8,128)(2,1)}, bf16[16,48,256]{2,1,0:T(8,128)(2,1)S(1)}, u32[]{:S(2)}) copy-start(bf16[16,48,256]{2,1,0:T(8,128)(2,1)S(1)} %broadcast_select_fusion.1.refs_0_) | copy-start | bytes 1179652
  109.1 35.4 %collective-permute-start.9 = (bf16[16,80,256]{2,1,0:T(8,128)(2,1)}, bf16[16,80,256]{2,1,0:T(8,128)(2,1)}, u32[]{:S(2)}, u32[]{:S(2)}) collective-permute-start(bf16[16,80,256]{2,1,0:T(8,128)(2,1)} %collective-permute-done.7.refs_0_), channel_id=1, source_target_pairs={{0,8},{8,0},{16,24},{24,16},{1,9},{9,1},{17,25},{25,17},{2,10},{10... | collective-permute-start | bytes 1966088 | tf_op jit(solution)/shard_map/ppermute | solution.py:362
  109.7 34.8 %collective-permute-start.11 = (bf16[16,80,256]{2,1,0:T(8,128)(2,1)}, bf16[16,80,256]{2,1,0:T(8,128)(2,1)}, u32[]{:S(2)}, u32[]{:S(2)}) collective-permute-start(bf16[16,80,256]{2,1,0:T(8,128)(2,1)} %collective-permute-done.1.refs_0_), channel_id=1, source_target_pairs={{0,16},{8,24},{16,0},{24,8},{1,17},{9,25},{17,1},{25,9},{2,18},{10... | collective-permute-start | bytes 1966088 | tf_op jit(solution)/shard_map/ppermute | solution.py:362
  119.7 2.2 copy-start.12
  119.7 22.5 %collective-permute-start.17 = (bf16[16,48,256]{2,1,0:T(8,128)(2,1)S(1)}, bf16[16,48,256]{2,1,0:T(8,128)(2,1)S(1)}, u32[]{:S(2)}, u32[]{:S(2)}) collective-permute-start(bf16[16,48,256]{2,1,0:T(8,128)(2,1)S(1)} %broadcast_select_fusion.1.refs_0_), channel_id=1, source_target_pairs={{0,16},{8,24},{16,0},{24,8},{1,17},{9,25},{17,1},{25,9},{2,18},{10... | collective-permute-start | bytes 1179656 | tf_op jit(solution)/shard_map/ppermute | solution.py:362
  121.2 0.7 copy-start.13
  121.2 35.1 %collective-permute-start.3 = (bf16[16,80,256]{2,1,0:T(8,128)(2,1)}, bf16[16,80,256]{2,1,0:T(8,128)(2,1)}, u32[]{:S(2)}, u32[]{:S(2)}) collective-permute-start(bf16[16,80,256]{2,1,0:T(8,128)(2,1)} %broadcast_select_fusion.refs_0_), channel_id=1, source_target_pairs={{0,16},{8,24},{16,0},{24,8},{1,17},{9,25},{17,1},{25,9},{2,18},{10... | collective-permute-start | bytes 1966088 | tf_op jit(solution)/shard_map/ppermute | solution.py:362
  121.8 34.6 %collective-permute-start.10 = (bf16[16,80,256]{2,1,0:T(8,128)(2,1)}, bf16[16,80,256]{2,1,0:T(8,128)(2,1)}, u32[]{:S(2)}, u32[]{:S(2)}) collective-permute-start(bf16[16,80,256]{2,1,0:T(8,128)(2,1)} %collective-permute-done.8.refs_1_), channel_id=1, source_target_pairs={{0,8},{8,0},{16,24},{24,16},{1,9},{9,1},{17,25},{25,17},{2,10},{10... | collective-permute-start | bytes 1966088 | tf_op jit(solution)/shard_map/ppermute | solution.py:362
  142.2 0.8 copy-start.7
  143.0 57.2 %collective-permute-start.29 = (bf16[1024,512]{1,0:T(8,128)(2,1)}, bf16[1024,512]{1,0:T(8,128)(2,1)}, u32[]{:S(2)}, u32[]{:S(2)}) collective-permute-start(bf16[1024,512]{1,0:T(8,128)(2,1)} %refs_4_.1), channel_id=1, source_target_pairs={{0,16},{8,24},{16,0},{24,8},{1,17},{9,25},{17,1},{25,9},{2,18},{10... | collective-permute-start | bytes 3145736 | tf_op jit(solution)/shard_map/ppermute | solution.py:362
  144.5 33.3 %collective-permute-start.12 = (bf16[16,80,256]{2,1,0:T(8,128)(2,1)}, bf16[16,80,256]{2,1,0:T(8,128)(2,1)}, u32[]{:S(2)}, u32[]{:S(2)}) collective-permute-start(bf16[16,80,256]{2,1,0:T(8,128)(2,1)} %collective-permute-done.1.refs_0_), channel_id=1, source_target_pairs={{0,8},{8,0},{16,24},{24,16},{1,9},{9,1},{17,25},{25,17},{2,10},{10... | collective-permute-start | bytes 1966088 | tf_op jit(solution)/shard_map/ppermute | solution.py:362
  144.5 33.4 %collective-permute-start.13 = (bf16[16,80,256]{2,1,0:T(8,128)(2,1)}, bf16[16,80,256]{2,1,0:T(8,128)(2,1)}, u32[]{:S(2)}, u32[]{:S(2)}) collective-permute-start(bf16[16,80,256]{2,1,0:T(8,128)(2,1)} %collective-permute-done.11.refs_1_), channel_id=1, source_target_pairs={{0,8},{8,0},{16,24},{24,16},{1,9},{9,1},{17,25},{25,17},{2,10},{10... | collective-permute-start | bytes 1966088 | tf_op jit(solution)/shard_map/ppermute | solution.py:362
  156.3 31.0 %collective-permute-start.4 = (bf16[16,80,256]{2,1,0:T(8,128)(2,1)}, bf16[16,80,256]{2,1,0:T(8,128)(2,1)}, u32[]{:S(2)}, u32[]{:S(2)}) collective-permute-start(bf16[16,80,256]{2,1,0:T(8,128)(2,1)} %broadcast_select_fusion.refs_0_), channel_id=1, source_target_pairs={{0,8},{8,0},{16,24},{24,16},{1,9},{9,1},{17,25},{25,17},{2,10},{10... | collective-permute-start | bytes 1966088 | tf_op jit(solution)/shard_map/ppermute | solution.py:362
  156.4 31.2 %collective-permute-start.5 = (bf16[16,80,256]{2,1,0:T(8,128)(2,1)}, bf16[16,80,256]{2,1,0:T(8,128)(2,1)}, u32[]{:S(2)}, u32[]{:S(2)}) collective-permute-start(bf16[16,80,256]{2,1,0:T(8,128)(2,1)} %collective-permute-done.3.refs_1_), channel_id=1, source_target_pairs={{0,8},{8,0},{16,24},{24,16},{1,9},{9,1},{17,25},{25,17},{2,10},{10... | collective-permute-start | bytes 1966088 | tf_op jit(solution)/shard_map/ppermute | solution.py:362
  177.8 9.8 %copy-start.8 = (bf16[16,48,256]{2,1,0:T(8,128)(2,1)S(1)}, bf16[16,48,256]{2,1,0:T(8,128)(2,1)}, u32[]{:S(2)}) copy-start(bf16[16,48,256]{2,1,0:T(8,128)(2,1)} %copy-done.7) | copy-start | bytes 1179652
  177.8 23.9 %collective-permute-start.23 = (bf16[16,48,256]{2,1,0:T(8,128)(2,1)}, bf16[16,48,256]{2,1,0:T(8,128)(2,1)}, u32[]{:S(2)}, u32[]{:S(2)}) collective-permute-start(bf16[16,48,256]{2,1,0:T(8,128)(2,1)} %collective-permute-done.21.refs_1_), channel_id=1, source_target_pairs={{0,8},{8,0},{16,24},{24,16},{1,9},{9,1},{17,25},{25,17},{2,10},{10... | collective-permute-start | bytes 1179656 | tf_op jit(solution)/shard_map/ppermute | solution.py:362
  177.9 23.8 %collective-permute-start.26 = (bf16[16,48,256]{2,1,0:T(8,128)(2,1)}, bf16[16,48,256]{2,1,0:T(8,128)(2,1)}, u32[]{:S(2)}, u32[]{:S(2)}) collective-permute-start(bf16[16,48,256]{2,1,0:T(8,128)(2,1)} %copy-done.12), channel_id=1, source_target_pairs={{0,8},{8,0},{16,24},{24,16},{1,9},{9,1},{17,25},{25,17},{2,10},{10... | collective-permute-start | bytes 1179656 | tf_op jit(solution)/shard_map/ppermute | solution.py:362
  187.4 29.0 %collective-permute-start.18 = (bf16[16,48,256]{2,1,0:T(8,128)(2,1)S(1)}, bf16[16,48,256]{2,1,0:T(8,128)(2,1)}, u32[]{:S(2)}, u32[]{:S(2)}) collective-permute-start(bf16[16,48,256]{2,1,0:T(8,128)(2,1)S(1)} %broadcast_select_fusion.1.refs_0_), channel_id=1, source_target_pairs={{0,8},{8,0},{16,24},{24,16},{1,9},{9,1},{17,25},{25,17},{2,10},{10... | collective-permute-start | bytes 1179656 | tf_op jit(solution)/shard_map/ppermute | solution.py:362
  187.5 28.8 %collective-permute-start.19 = (bf16[16,48,256]{2,1,0:T(8,128)(2,1)S(1)}, bf16[16,48,256]{2,1,0:T(8,128)(2,1)}, u32[]{:S(2)}, u32[]{:S(2)}) collective-permute-start(bf16[16,48,256]{2,1,0:T(8,128)(2,1)S(1)} %copy-done.8), channel_id=1, source_target_pairs={{0,8},{8,0},{16,24},{24,16},{1,9},{9,1},{17,25},{25,17},{2,10},{10... | collective-permute-start | bytes 1179656 | tf_op jit(solution)/shard_map/ppermute | solution.py:362
  200.1 47.9 %collective-permute-start.27 = (bf16[5120,128]{1,0:T(8,128)(2,1)}, bf16[5120,128]{1,0:T(8,128)(2,1)}, u32[]{:S(2)}, u32[]{:S(2)}) collective-permute-start(bf16[5120,128]{1,0:T(8,128)(2,1)} %get-tuple-element.23), channel_id=1, source_target_pairs={{0,1},{1,0},{2,3},{3,2},{4,5},{5,4},{6,7},{7,6},{8,9},{9,8},{10,11... | collective-permute-start | bytes 3932168 | tf_op jit(solution)/shard_map/ppermute | solution.py:362
  201.7 26.5 %collective-permute-start.30 = (bf16[1024,512]{1,0:T(8,128)(2,1)}, bf16[1024,512]{1,0:T(8,128)(2,1)}, u32[]{:S(2)}, u32[]{:S(2)}) collective-permute-start(bf16[1024,512]{1,0:T(8,128)(2,1)} %refs_4_.1), channel_id=1, source_target_pairs={{0,8},{8,0},{16,24},{24,16},{1,9},{9,1},{17,25},{25,17},{2,10},{10... | collective-permute-start | bytes 3145736 | tf_op jit(solution)/shard_map/ppermute | solution.py:362
  201.7 26.5 %collective-permute-start.31 = (bf16[1024,512]{1,0:T(8,128)(2,1)}, bf16[1024,512]{1,0:T(8,128)(2,1)}, u32[]{:S(2)}, u32[]{:S(2)}) collective-permute-start(bf16[1024,512]{1,0:T(8,128)(2,1)} %collective-permute-done.29.refs_5_), channel_id=1, source_target_pairs={{0,8},{8,0},{16,24},{24,16},{1,9},{9,1},{17,25},{25,17},{2,10},{10... | collective-permute-start | bytes 3145736 | tf_op jit(solution)/shard_map/ppermute | solution.py:362
  216.3 11.0 %copy-start.10 = (bf16[4,32,128]{2,1,0:T(8,128)(2,1)S(1)}, bf16[4,32,128]{2,1,0:T(8,128)(2,1)}, u32[]{:S(2)}) copy-start(bf16[4,32,128]{2,1,0:T(8,128)(2,1)} %param.8) | copy-start | bytes 98308
  226.7 21.3 %collective-permute-start.28 = (bf16[3072,128]{1,0:T(8,128)(2,1)}, bf16[3072,128]{1,0:T(8,128)(2,1)S(1)}, u32[]{:S(2)}, u32[]{:S(2)}) collective-permute-start(bf16[3072,128]{1,0:T(8,128)(2,1)} %get-tuple-element.24), channel_id=1, source_target_pairs={{0,1},{1,0},{2,3},{3,2},{4,5},{5,4},{6,7},{7,6},{8,9},{9,8},{10,11... | collective-permute-start | bytes 2359304 | tf_op jit(solution)/shard_map/ppermute | solution.py:362
  248.0 1.7 copy-start.1
  249.8 1.4 copy-start.3
